TPU v7x, 32 devices: a whole 2x2x4 slice. The times are simulated.
32 devices in a mesh: tm: 4 (over z), ent: 8 (over y, x, core).
Axes of the slice: x: 2, y: 2, z: 4, core: 2. Of those that a mesh axis runs over, the one named last changes fastest.
Arguments:
- states: bfloat16 [4, 8192, 512], P('tm', 'ent'), may hold values from -6 to 6
- cotangent: bfloat16 [4, 8192, 512], P('tm', 'ent'), may hold values from -6 to 6
- export_rows: int32 [4, 2048], P('tm', 'ent'), may hold values from 0 to 1023
- edge_src: int32 [4, 8192], P('tm', 'ent'), may hold values from 0 to 255
- edge_dst: int32 [4, 8192], P('tm', 'ent'), may hold values from 0 to 1023
- edge_rel: int32 [4, 8192], P('tm', 'ent'), may hold values from 0 to 255
- tile_count: int32 [4, 8], P('tm', 'ent'), may hold values from 1 to 8, as said below
- basis: bfloat16 [512, 2048], replicated, may hold values from -0.25 to 0.25
- coef: float32 [256, 4], replicated, may hold values from -3 to 3
- rel_emb: bfloat16 [256, 512], replicated, may hold values from -3 to 3
- self_weight: bfloat16 [512, 512], replicated, may hold values from -0.25 to 0.25
- gate_weight: bfloat16 [512, 512], replicated, may hold values from -0.25 to 0.25
- gate_bias: float32 [512], replicated, may hold values from -2 to 1
Outputs:
- grad_states: float32 [4, 8192, 512], P('tm', 'ent')
- grad_basis: float32 [512, 2048], P('ent')
- grad_self: float32 [512, 512], P('ent')
- grad_gate: float32 [512, 512], P('ent')
- grad_gate_bias: float32 [512], P('ent')
- grad_coef: float32 [256, 4], P('ent')
- grad_rel_emb: float32 [256, 512], P('ent')
Inputs may be any that keep to these rules, and one draw needn't show every extreme that they name: `tile_count`: some slab of some snapshot has 8 live tiles in every draw.
All inputs are finite; a program needn't handle non-finite values.
Results may differ from a plain program's by a relative error of at most 0.01.
Values may be sent and summed in bfloat16 or wider, within the bound.
No kernel may reach another device: no remote copies, remote signals or barrier semaphores. Data moves between devices by JAX's collectives and lax.ppermute only.
A program may use at most 128 MiB of HBM per device.

v0:
```python
import jax
import jax.numpy as jnp
from jax import lax
from jax.sharding import PartitionSpec as P

TILE = 128


def shifted(block, axis, distance):
    devices = range(lax.axis_size(axis))
    route = [(i - distance, i) for i in devices if i - distance in devices]
    return lax.ppermute(block, axis, route)


def per_device(
    states,
    cotangent,
    export_rows,
    edge_src,
    edge_dst,
    edge_rel,
    tile_count,
    basis,
    coef,
    rel_emb,
    self_weight,
    gate_weight,
    gate_bias,
):
    ent_count = lax.axis_size("ent")
    section_count = lax.axis_size("tm")
    own_state = states[0]
    row_count, feature_width = own_state.shape
    basis_count = basis.shape[1] // feature_width
    relation_count = rel_emb.shape[0]
    exported_rows = export_rows[0]
    edge_source = edge_src[0]
    edge_target = edge_dst[0]
    edge_count = edge_source.shape[0]
    slot_count = exported_rows.shape[0]
    live_mask = jnp.arange(edge_count, dtype=jnp.int32) // TILE < tile_count[0, 0]
    rel_onehot = (
        edge_rel[0][:, None] == jnp.arange(relation_count, dtype=jnp.int32)[None, :]
    ).astype(jnp.float32)
    received = lax.all_to_all(
        own_state[exported_rows], "ent", split_axis=0, concat_axis=0, tiled=True
    )
    rel_rows = jnp.dot(rel_onehot.astype(jnp.bfloat16), rel_emb, preferred_element_type=jnp.float32)
    edge_input = (received[edge_source].astype(jnp.float32) + rel_rows).astype(jnp.bfloat16)
    images = jnp.dot(edge_input, basis, preferred_element_type=jnp.float32).reshape(
        edge_count, basis_count, feature_width
    )
    edge_coef = jnp.dot(rel_onehot, coef, precision=lax.Precision.HIGHEST)
    message = jnp.einsum("eb,ebd->ed", edge_coef, images)
    message = jnp.where(live_mask[:, None], message, jnp.zeros((), jnp.float32))
    degree = 1.0 + jax.ops.segment_sum(live_mask.astype(jnp.float32), edge_target, row_count)
    self_part = jnp.dot(own_state, self_weight, preferred_element_type=jnp.float32)
    summed = (jax.ops.segment_sum(message, edge_target, row_count) + self_part) / degree[:, None]
    aggregated = jnp.tanh(summed)
    gate_open = jax.nn.sigmoid(
        jnp.dot(own_state, gate_weight, preferred_element_type=jnp.float32) + gate_bias
    )
    state_float = own_state.astype(jnp.float32)
    handed = jnp.zeros((row_count, feature_width), jnp.bfloat16)
    contract_last = (((1,), (1,)), ((), ()))
    contract_first = (((0,), (0,)), ((), ()))
    for section_step in range(section_count):
        upstream = cotangent[0].astype(jnp.float32) + handed.astype(jnp.float32)
        row_grad = (
            upstream * gate_open * (1.0 - aggregated * aggregated) / degree[:, None]
        ).astype(jnp.bfloat16)
        gate_grad = upstream * (aggregated - state_float) * gate_open * (1.0 - gate_open)
        gate_row = gate_grad.astype(jnp.bfloat16)
        edge_grad = jnp.where(
            live_mask[:, None], row_grad[edge_target], jnp.zeros((), jnp.bfloat16)
        )
        image_grad = (
            (edge_coef[:, :, None] * edge_grad.astype(jnp.float32)[:, None, :])
            .astype(jnp.bfloat16)
            .reshape(edge_count, basis_count * feature_width)
        )
        input_grad = lax.dot_general(
            image_grad, basis, contract_last, preferred_element_type=jnp.float32
        )
        slot_grad = jax.ops.segment_sum(input_grad, edge_source, slot_count)
        returned = lax.all_to_all(slot_grad, "ent", split_axis=0, concat_axis=0, tiled=True)
        state_grad = upstream * (1.0 - gate_open)
        state_grad = state_grad + lax.dot_general(
            row_grad, self_weight, contract_last, preferred_element_type=jnp.float32
        )
        state_grad = state_grad + lax.dot_general(
            gate_row, gate_weight, contract_last, preferred_element_type=jnp.float32
        )
        state_grad = state_grad + jax.ops.segment_sum(returned, exported_rows, row_count)
        if section_step + 1 < section_count:
            handed = shifted(state_grad.astype(jnp.bfloat16), "tm", -1)
    basis_term = lax.dot_general(
        edge_input, image_grad, contract_first, preferred_element_type=jnp.float32
    )
    self_term = lax.dot_general(
        own_state, row_grad, contract_first, preferred_element_type=jnp.float32
    )
    gate_term = lax.dot_general(
        own_state, gate_row, contract_first, preferred_element_type=jnp.float32
    )
    bias_term = jnp.sum(gate_grad, axis=0)
    coef_edge = jnp.einsum("ed,ebd->eb", edge_grad.astype(jnp.float32), images)
    coef_term = lax.dot_general(
        rel_onehot, coef_edge, contract_first, precision=lax.Precision.HIGHEST
    )
    relation_term = lax.dot_general(
        rel_onehot, input_grad, contract_first, precision=lax.Precision.HIGHEST
    )
    summed_terms = lax.psum(
        (basis_term, self_term, gate_term, bias_term, coef_term, relation_term), ("tm", "ent")
    )
    slab_index = lax.axis_index("ent")
    final_parts = tuple(
        (
            lax.dynamic_slice_in_dim(
                matrix_term,
                slab_index * (matrix_term.shape[0] // ent_count),
                matrix_term.shape[0] // ent_count,
                0,
            )
            for matrix_term in summed_terms
        )
    )
    return (
        state_grad[None],
        final_parts[0],
        final_parts[1],
        final_parts[2],
        final_parts[3],
        final_parts[4],
        final_parts[5],
    )


def solution(mesh):
    placed = (
        P("tm", "ent", None),
        P("tm", "ent", None),
        P("tm", "ent"),
        P("tm", "ent"),
        P("tm", "ent"),
        P("tm", "ent"),
        P("tm", "ent"),
        P(),
        P(),
        P(),
        P(),
        P(),
        P(),
    )
    return jax.shard_map(
        per_device,
        mesh=mesh,
        in_specs=placed,
        out_specs=(
            P("tm", "ent", None),
            P("ent", None),
            P("ent", None),
            P("ent", None),
            P("ent"),
            P("ent", None),
            P("ent", None),
        ),
        check_vma=False,
    )
```

profile of v0, /device:TPU:0, one launch (start us, length us, event | category | flops | bytes accessed | tf_op | source)
XLA Modules:
  0.0 496.6 jit_solution(8023949450822528432)
XLA Ops:
  11.4 5.3 %all-to-all-start = ((bf16[8,32,512]{2,1,0:T(8,128)(2,1)}), bf16[8,32,512]{2,1,0:T(8,128)(2,1)S(1)}, u32[]{:S(2)}, u32[]{:S(2)}) async-start(bf16[8,32,512]{2,1,0:T(8,128)(2,1)} %bitcast.144), calls=%async_computation | async-start | bytes 524288 | tf_op jit(solution)/shard_map/all_to_all | solution.py:45
  23.4 7.8 %scatter_custom_fusion.1 = f32[1024]{0:T(1024)S(1)} fusion(s32[1024]{0:T(1024)S(1)} %bitcast.158, f32[1024]{0:T(1024)S(1)} %get-tuple-element.35, f32[]{:T(128)} %constant.14.clone.1), kind=kCustom, calls=%fused_computation.105 | custom fusion | flops 1024 | bytes 4100 | tf_op jit(solution)/shard_map/scatter-add | solution.py:56
  42.1 7.9 %reshape.211 = bf16[1024,4,512]{2,1,0:T(4,128)(2,1)} reshape(bf16[1024,2048]{1,0:T(8,128)(2,1)} %fusion.64) | data formatting | bytes 8388608 | tf_op jit(solution)/shard_map/reshape | solution.py:50
  50.0 5.9 %fusion.65 = f32[1024,1,512]{2,1,0:T(1,128)} fusion(bf16[1024,4,1]{1,2,0:T(2,128)(2,1)S(1)} %copy-done.30, bf16[1024,4,512]{2,1,0:T(4,128)(2,1)} %reshape.211), kind=kOutput, calls=%fused_computation.126 | convolution fusion | flops 4194304 | bytes 6299648 | tf_op jit(solution)/shard_map/eb,ebd->ed/dot_general | solution.py:54
  55.8 11.4 %scatter_custom_fusion = f32[1024,512]{1,0:T(8,128)} fusion(f32[1024,512]{1,0:T(8,128)} %fusion.57, s32[1024]{0:T(1024)S(1)} %bitcast.159, f32[1024,1,512]{2,1,0:T(1,128)} %fusion.65, f32[]{:T(128)} %constant.22.clone.1, pred[1024]{0:T(1024)(128)(4,1)S(1)} %get-tuple-element.34), kind=kCustom, calls=%fused_computation.35 | custom fusion | flops 1048576 | bytes 4195840 | tf_op jit(solution)/shard_map/scatter-add | solution.py:58
  67.2 5.2 %fusion.4 = (bf16[1024,512]{1,0:T(8,128)(2,1)S(1)}, f32[1024,512]{1,0:T(8,128)}) fusion(bf16[1,1024,512]{2,1,0:T(8,128)(2,1)} %param.14, f32[1024]{0:T(1024)S(1)} %scatter_custom_fusion.1, f32[1024,512]{1,0:T(8,128)} %scatter_custom_fusion, f32[512]{0:T(512)S(1)} %copy-done.36, bf16[512,512]{1,0:T(8,128)(2,1)} %param.24, bf16[1,1024,512]{2,1,0:T(8,128)(2,1)} %param.13), kind=kOutput, calls=%fused_computation.30 | convolution fusion | flops 543162368 | bytes 7870464 | tf_op jit(solution)/shard_map/dot_general | solution.py:61
  88.2 8.0 %scatter_custom_fusion.2 = f32[256,512]{1,0:T(8,128)} fusion(s32[1024]{0:T(1024)S(1)} %bitcast.160, f32[1024,512]{1,0:T(8,128)} %fusion.67, f32[]{:T(128)} %constant.22.clone.1), kind=kCustom, calls=%fused_computation.89 | custom fusion | flops 524288 | bytes 524800 | tf_op jit(solution)/shard_map/scatter-add | solution.py:85
  100.4 6.4 %fusion.1 = f32[1024,512]{1,0:T(8,128)} fusion(f32[1024,512]{1,0:T(8,128)} %fusion.66, bf16[512,512]{1,0:T(8,128)(2,1)} %param.24, f32[1024,512]{1,0:T(8,128)} %get-tuple-element.33, bf16[1,1024,512]{2,1,0:T(8,128)(2,1)S(1)} %copy-done.5, bf16[1,1024,512]{2,1,0:T(8,128)(2,1)} %param.13, f32[1024,512]{1,0:T(8,128)} %scatter_custom_fusion, ...), kind=kOutput, calls=%fused_computation.27 | convolution fusion | flops 544210944 | bytes 11014144 | tf_op jit(solution)/shard_map/dot_general | solution.py:91
  110.2 5.9 %scatter_fusion = f32[1024,512]{1,0:T(8,128)} fusion(f32[1024,512]{1,0:T(8,128)} %fusion.1, s32[256]{0:T(256)S(1)} %bitcast.151, f32[256,512]{1,0:T(8,128)} %bitcast.19), kind=kCustom, calls=%fused_computation.9 | custom fusion | flops 131072 | bytes 1573888 | tf_op jit(solution)/shard_map/scatter-add | solution.py:94
  119.4 23.2 %collective-permute-done = bf16[1024,512]{1,0:T(8,128)(2,1)S(1)} collective-permute-done((bf16[1024,512]{1,0:T(8,128)(2,1)S(1)}, bf16[1024,512]{1,0:T(8,128)(2,1)S(1)}, u32[]{:S(2)}, u32[]{:S(2)}) %collective-permute-start) | collective-permute-done | bytes 1048608 | tf_op jit(solution)/shard_map/ppermute | solution.py:12
  146.0 5.1 %gather_fusion.3 = bf16[1024,512]{1,0:T(8,128)(2,1)} fusion(bf16[1024,512]{1,0:T(8,128)(2,1)S(1)} %divide_convert_fusion.2, s32[1024]{0:T(1024)S(1)} %broadcast_clamp_fusion.1), kind=kCustom, calls=%fused_computation.3 | custom fusion | bytes 2101248 | tf_op jit(solution)/shard_map/gather | solution.py:75
  162.5 8.0 %scatter_custom_fusion.4 = f32[256,512]{1,0:T(8,128)} fusion(s32[1024]{0:T(1024)S(1)} %bitcast.161, f32[1024,512]{1,0:T(8,128)} %fusion.69, f32[]{:T(128)} %constant.22.clone.1), kind=kCustom, calls=%fused_computation.87 | custom fusion | flops 524288 | bytes 524800 | tf_op jit(solution)/shard_map/scatter-add | solution.py:85
  175.1 7.3 %add_add_fusion.2 = f32[1024,512]{1,0:T(8,128)} fusion(f32[1024,512]{1,0:T(8,128)} %fusion.68, bf16[1024,512]{1,0:T(8,128)(2,1)} %copy-done.28, f32[1024,512]{1,0:T(8,128)} %get-tuple-element.33, bf16[512,512]{1,0:T(8,128)(2,1)} %param.24, bf16[1,1024,512]{2,1,0:T(8,128)(2,1)S(1)} %copy-done.7, bf16[1,1024,512]{2,1,0:T(8,128)(2,1)} %param.13, ...), kind=kOutput, calls=%fused_computation.46 | convolution fusion | flops 546308096 | bytes 12062720 | tf_op jit(solution)/shard_map/dot_general | solution.py:91
  184.8 5.5 %scatter_fusion.1 = f32[1024,512]{1,0:T(8,128)} fusion(f32[1024,512]{1,0:T(8,128)} %add_add_fusion.2, s32[256]{0:T(256)S(1)} %bitcast.152, f32[256,512]{1,0:T(8,128)} %bitcast.21), kind=kCustom, calls=%fused_computation.11 | custom fusion | flops 131072 | bytes 1573888 | tf_op jit(solution)/shard_map/scatter-add | solution.py:94
  193.5 23.7 %collective-permute-done.1 = bf16[1024,512]{1,0:T(8,128)(2,1)S(1)} collective-permute-done((bf16[1024,512]{1,0:T(8,128)(2,1)S(1)}, bf16[1024,512]{1,0:T(8,128)(2,1)S(1)}, u32[]{:S(2)}, u32[]{:S(2)}) %collective-permute-start.1) | collective-permute-done | bytes 1048608 | tf_op jit(solution)/shard_map/ppermute | solution.py:12
  237.0 8.2 %scatter_custom_fusion.6 = f32[256,512]{1,0:T(8,128)} fusion(s32[1024]{0:T(1024)S(1)} %bitcast.162, f32[1024,512]{1,0:T(8,128)} %fusion.71, f32[]{:T(128)} %constant.22.clone.1), kind=kCustom, calls=%fused_computation.85 | custom fusion | flops 524288 | bytes 524800 | tf_op jit(solution)/shard_map/scatter-add | solution.py:85
  249.5 7.3 %add_add_fusion.1 = f32[1024,512]{1,0:T(8,128)} fusion(f32[1024,512]{1,0:T(8,128)} %fusion.70, bf16[1024,512]{1,0:T(8,128)(2,1)} %copy-done.27, f32[1024,512]{1,0:T(8,128)} %get-tuple-element.33, bf16[512,512]{1,0:T(8,128)(2,1)} %param.24, bf16[1,1024,512]{2,1,0:T(8,128)(2,1)S(1)} %copy-done.9, bf16[1,1024,512]{2,1,0:T(8,128)(2,1)} %param.13, ...), kind=kOutput, calls=%fused_computation.43 | convolution fusion | flops 546308096 | bytes 12062720 | tf_op jit(solution)/shard_map/dot_general | solution.py:91
  259.1 5.5 %scatter_fusion.2 = f32[1024,512]{1,0:T(8,128)} fusion(f32[1024,512]{1,0:T(8,128)} %add_add_fusion.1, s32[256]{0:T(256)S(1)} %bitcast.153, f32[256,512]{1,0:T(8,128)} %bitcast.23), kind=kCustom, calls=%fused_computation.13 | custom fusion | flops 131072 | bytes 1573888 | tf_op jit(solution)/shard_map/scatter-add | solution.py:94
  267.8 23.6 %collective-permute-done.2 = bf16[1024,512]{1,0:T(8,128)(2,1)S(1)} collective-permute-done((bf16[1024,512]{1,0:T(8,128)(2,1)S(1)}, bf16[1024,512]{1,0:T(8,128)(2,1)S(1)}, u32[]{:S(2)}, u32[]{:S(2)}) %collective-permute-start.2) | collective-permute-done | bytes 1048608 | tf_op jit(solution)/shard_map/ppermute | solution.py:12
  319.3 8.3 %scatter_custom_fusion.8 = f32[256,512]{1,0:T(8,128)} fusion(s32[1024]{0:T(1024)S(1)} %bitcast.163, f32[1024,512]{1,0:T(8,128)} %copy-done.26, f32[]{:T(128)} %constant.22.clone.1), kind=kCustom, calls=%fused_computation.83 | custom fusion | flops 524288 | bytes 524800 | tf_op jit(solution)/shard_map/scatter-add | solution.py:85
  331.7 6.3 %fusion.9 = f32[1024,1,4]{2,1,0:T(1,128)S(1)} fusion(bf16[1024,4,512]{2,1,0:T(4,128)(2,1)} %reshape.211, bf16[1024,512,1]{1,0,2:T(8,128)(2,1)} %get-tuple-element.30), kind=kOutput, calls=%fused_computation.36 | convolution fusion | flops 4194304 | bytes 5259264 | tf_op jit(solution)/shard_map/ed,ebd->eb/dot_general | solution.py:107
  338.7 41.7 %all-reduce = (f32[512]{0:T(512)S(1)}, f32[256,4]{0,1:T(4,128)S(1)}) all-reduce(f32[512]{0:T(512)S(1)} %get-tuple-element.27, f32[256,4]{0,1:T(4,128)S(1)} %fusion.20), channel_id=1, replica_groups=mesh['tm'=4,'ent'=8] {'tm','ent'}, use_global_device_ids=true, to_apply=%region_14.15 | all-reduce | flops 1536 | bytes 12288 | tf_op jit(solution)/shard_map/psum | solution.py:114
  387.2 5.5 %scatter_fusion.3 = f32[1024,512]{1,0:T(8,128)} fusion(f32[1024,512]{1,0:T(8,128)} %add_add_fusion, s32[256]{0:T(256)S(1)} %bitcast.154, f32[256,512]{1,0:T(8,128)} %bitcast.25), kind=kCustom, calls=%fused_computation.15 | custom fusion | flops 131072 | bytes 1573888 | tf_op jit(solution)/shard_map/scatter-add | solution.py:94
  392.7 89.6 %all-reduce.4.cloned.1.call-done = (f32[512,2048]{1,0:T(8,128)}, f32[512,512]{0,1:T(8,128)}, f32[512,512]{0,1:T(8,128)}, f32[256,512]{1,0:T(8,128)}) async-done(((f32[512,2048]{1,0:T(8,128)}, f32[512,512]{0,1:T(8,128)}, f32[512,512]{0,1:T(8,128)}, f32[256,512]{1,0:T(8,128)}), (f32[512,2048]{1,0:T(8,128)}, f32[512,512]{0,1:T(8,128)}, f32[512,512]{0,1:T(8,128)}, ...) | async-done | bytes 6815760 | tf_op jit(solution)/shard_map/psum | solution.py:114
  (146 shorter events, 148.6 us)
Async XLA Ops:
  7.2 30.6 %copy-start = (bf16[512,2048]{1,0:T(8,128)(2,1)S(1)}, bf16[512,2048]{1,0:T(8,128)(2,1)}, u32[]{:S(2)}) copy-start(bf16[512,2048]{1,0:T(8,128)(2,1)} %param.20) | copy-start | bytes 6291460
  7.2 10.2 %copy-start.12 = (bf16[1,1024,512]{2,1,0:T(8,128)(2,1)S(1)}, bf16[1,1024,512]{2,1,0:T(8,128)(2,1)}, u32[]{:S(2)}) copy-start(bf16[1,1024,512]{2,1,0:T(8,128)(2,1)} %param.13) | copy-start | bytes 3145732
  7.2 10.2 %copy-start.34 = (s32[1,1024]{1,0:T(1,128)S(1)}, s32[1,1024]{1,0:T(1,128)}, u32[]{:S(2)}) copy-start(s32[1,1024]{1,0:T(1,128)} %param.16) | copy-start | bytes 12292
  7.2 10.2 %copy-start.33 = (s32[1,1024]{1,0:T(1,128)S(1)}, s32[1,1024]{1,0:T(1,128)}, u32[]{:S(2)}) copy-start(s32[1,1024]{1,0:T(1,128)} %param.17) | copy-start | bytes 12292
  11.4 19.9 %all-to-all-start = ((bf16[8,32,512]{2,1,0:T(8,128)(2,1)}), bf16[8,32,512]{2,1,0:T(8,128)(2,1)S(1)}, u32[]{:S(2)}, u32[]{:S(2)}) async-start(bf16[8,32,512]{2,1,0:T(8,128)(2,1)} %bitcast.144), calls=%async_computation | async-start | bytes 524288 | tf_op jit(solution)/shard_map/all_to_all | solution.py:45
  55.8 11.4 %copy-start.36 = (f32[512]{0:T(512)S(1)}, f32[512]{0:T(512)}, u32[]{:S(2)}) copy-start(f32[512]{0:T(512)} %param.25) | copy-start | bytes 6148
  84.4 16.0 %copy-start.5 = (bf16[1,1024,512]{2,1,0:T(8,128)(2,1)S(1)}, bf16[1,1024,512]{2,1,0:T(8,128)(2,1)}, u32[]{:S(2)}) copy-start(bf16[1,1024,512]{2,1,0:T(8,128)(2,1)} %param.14) | copy-start | bytes 3145732
  96.2 14.0 %all-to-all-start.1 = ((f32[8,32,512]{2,1,0:T(8,128)}), f32[8,32,512]{2,1,0:T(8,128)}, u32[]{:S(2)}, u32[]{:S(2)}) async-start(f32[8,32,512]{2,1,0:T(8,128)} %bitcast.142), calls=%async_computation.1 | async-start | bytes 1048576 | tf_op jit(solution)/shard_map/all_to_all | solution.py:86
  100.4 9.8 %copy-start.32 = (s32[1,256]{1,0:T(1,128)S(1)}, s32[1,256]{1,0:T(1,128)}, u32[]{:S(2)}) copy-start(s32[1,256]{1,0:T(1,128)} %param.15) | copy-start | bytes 3076
  116.2 27.4 %copy-start.1 = (f32[1024,512]{1,0:T(8,128)S(1)}, f32[1024,512]{1,0:T(8,128)}, u32[]{:S(2)}) copy-start(f32[1024,512]{1,0:T(8,128)} %get-tuple-element.33) | copy-start | bytes 6291460
  116.2 27.4 %copy-start.6 = (bf16[1,1024,512]{2,1,0:T(8,128)(2,1)S(1)}, bf16[1,1024,512]{2,1,0:T(8,128)(2,1)}, u32[]{:S(2)}) copy-start(bf16[1,1024,512]{2,1,0:T(8,128)(2,1)} %param.14) | copy-start | bytes 3145732
  118.1 24.5 %collective-permute-start = (bf16[1024,512]{1,0:T(8,128)(2,1)S(1)}, bf16[1024,512]{1,0:T(8,128)(2,1)S(1)}, u32[]{:S(2)}, u32[]{:S(2)}) collective-permute-start(bf16[1024,512]{1,0:T(8,128)(2,1)S(1)} %convert_element_type.141), channel_id=1, source_target_pairs={{8,0},{16,8},{24,16},{9,1},{17,9},{25,17},{10,2},{18,10},{26,18},{... | collective-permute-start | bytes 3145736 | tf_op jit(solution)/shard_map/ppermute | solution.py:12
  158.7 16.3 %copy-start.7 = (bf16[1,1024,512]{2,1,0:T(8,128)(2,1)S(1)}, bf16[1,1024,512]{2,1,0:T(8,128)(2,1)}, u32[]{:S(2)}) copy-start(bf16[1,1024,512]{2,1,0:T(8,128)(2,1)} %param.14) | copy-start | bytes 3145732
  170.5 14.3 %all-to-all-start.2 = ((f32[8,32,512]{2,1,0:T(8,128)}), f32[8,32,512]{2,1,0:T(8,128)}, u32[]{:S(2)}, u32[]{:S(2)}) async-start(f32[8,32,512]{2,1,0:T(8,128)} %bitcast.143), calls=%async_computation.2 | async-start | bytes 1048576 | tf_op jit(solution)/shard_map/all_to_all | solution.py:86
  190.3 27.9 %copy-start.2 = (f32[1024,512]{1,0:T(8,128)S(1)}, f32[1024,512]{1,0:T(8,128)}, u32[]{:S(2)}) copy-start(f32[1024,512]{1,0:T(8,128)} %get-tuple-element.33) | copy-start | bytes 6291460
  190.3 27.9 %copy-start.8 = (bf16[1,1024,512]{2,1,0:T(8,128)(2,1)S(1)}, bf16[1,1024,512]{2,1,0:T(8,128)(2,1)}, u32[]{:S(2)}) copy-start(bf16[1,1024,512]{2,1,0:T(8,128)(2,1)} %param.14) | copy-start | bytes 3145732
  192.2 25.0 %collective-permute-start.1 = (bf16[1024,512]{1,0:T(8,128)(2,1)S(1)}, bf16[1024,512]{1,0:T(8,128)(2,1)S(1)}, u32[]{:S(2)}, u32[]{:S(2)}) collective-permute-start(bf16[1024,512]{1,0:T(8,128)(2,1)S(1)} %convert_element_type.148), channel_id=1, source_target_pairs={{8,0},{16,8},{24,16},{9,1},{17,9},{25,17},{10,2},{18,10},{26,18},{... | collective-permute-start | bytes 3145736 | tf_op jit(solution)/shard_map/ppermute | solution.py:12
  233.3 16.2 %copy-start.9 = (bf16[1,1024,512]{2,1,0:T(8,128)(2,1)S(1)}, bf16[1,1024,512]{2,1,0:T(8,128)(2,1)}, u32[]{:S(2)}) copy-start(bf16[1,1024,512]{2,1,0:T(8,128)(2,1)} %param.14) | copy-start | bytes 3145732
  245.3 13.9 %all-to-all-start.3 = ((f32[8,32,512]{2,1,0:T(8,128)}), f32[8,32,512]{2,1,0:T(8,128)}, u32[]{:S(2)}, u32[]{:S(2)}) async-start(f32[8,32,512]{2,1,0:T(8,128)} %bitcast.141), calls=%async_computation.3 | async-start | bytes 1048576 | tf_op jit(solution)/shard_map/all_to_all | solution.py:86
  249.4 232.9 %all-reduce.4.cloned.1.call-start = ((), (), s32[]{:S(2)}) async-start(), calls=%async_computation.5 | async-start | bytes 13631488 | tf_op jit(solution)/shard_map/psum | solution.py:114
  264.6 26.8 %copy-start.3 = (f32[1024,512]{1,0:T(8,128)S(1)}, f32[1024,512]{1,0:T(8,128)}, u32[]{:S(2)}) copy-start(f32[1024,512]{1,0:T(8,128)} %get-tuple-element.33) | copy-start | bytes 6291460
  264.6 26.8 %copy-start.10 = (bf16[1,1024,512]{2,1,0:T(8,128)(2,1)S(1)}, bf16[1,1024,512]{2,1,0:T(8,128)(2,1)}, u32[]{:S(2)}) copy-start(bf16[1,1024,512]{2,1,0:T(8,128)(2,1)} %param.14) | copy-start | bytes 3145732
  266.5 24.9 %collective-permute-start.2 = (bf16[1024,512]{1,0:T(8,128)(2,1)S(1)}, bf16[1024,512]{1,0:T(8,128)(2,1)S(1)}, u32[]{:S(2)}, u32[]{:S(2)}) collective-permute-start(bf16[1024,512]{1,0:T(8,128)(2,1)S(1)} %convert_element_type.155), channel_id=1, source_target_pairs={{8,0},{16,8},{24,16},{9,1},{17,9},{25,17},{10,2},{18,10},{26,18},{... | collective-permute-start | bytes 3145736 | tf_op jit(solution)/shard_map/ppermute | solution.py:12
  327.6 59.7 %all-to-all-start.4 = ((f32[8,32,512]{2,1,0:T(8,128)}), f32[8,32,512]{2,1,0:T(8,128)}, u32[]{:S(2)}, u32[]{:S(2)}) async-start(f32[8,32,512]{2,1,0:T(8,128)} %bitcast.140), calls=%async_computation.4 | async-start | bytes 1048576 | tf_op jit(solution)/shard_map/all_to_all | solution.py:86
  (22 other events, 79.6 us)
Sparse Core Ops, SparseCore 0:
  319.4 162.8 all-reduce.3
where the time goes:
time: 502 us; the launch traced here: 497 us
  waiting for transfers between devices  168 us (33%)
  other arithmetic  101 us (20%)
  matrix products  87.5 us (17%)
  local copies, waits for them, and re-layouts  56.4 us (11%)
  blocking collectives  41.7 us (8%)
  starting transfers between devices  26.3 us (5%)
  between operations  15.7 us (3%)
    psum x1, waiting for transfers between devices, per_device(): lax.psum((basis_term, self_term, gate_term, bias_term, coef_term, relatio...  89.6 us
    ppermute x3, waiting for transfers between devices, shifted(): return lax.ppermute(block, axis, route)  70.5 us
    psum x1, blocking collectives, per_device(): lax.psum((basis_term, self_term, gate_term, bias_term, coef_term, relatio...  41.7 us
    scatter-add x4, other arithmetic, per_device(): slot_grad = jax.ops.segment_sum(input_grad, edge_source, slot_count)  32.6 us
    dot_general x4, matrix products, per_device(): lax.dot_general(gate_row, gate_weight, contract_last, preferred_element_t...  24.7 us
    scatter-add x4, other arithmetic, per_device(): jax.ops.segment_sum(returned, exported_rows, row_count)  22.4 us
    gather x4, local copies, waits for them, and re-layouts, per_device(): row_grad[edge_target]  20.3 us
    all_to_all x4, starting transfers between devices, per_device(): lax.all_to_all(slot_grad, 'ent', split_axis=0, concat_axis=0, tiled=True)  17 us
  transfers between devices with their start and end apart: 9, of which 7 were waited for; matrix products, arithmetic and copies ran while one was open for 13% of the time, Pallas kernels for 0%

commit v1 on v0

v1 whole, which is shorter than its diff:
```python
import functools

import jax
import jax.numpy as jnp
from jax import lax
from jax.experimental import pallas as pl
from jax.experimental.pallas import tpu as pltpu
from jax.sharding import PartitionSpec as P

TILE = 128
LANES = 128
BF = jnp.bfloat16
F32 = jnp.float32
VM = pltpu.VMEM


def dot(left, right, left_dim=1, right_dim=0):
    return lax.dot_general(
        left, right, (((left_dim,), (right_dim,)), ((), ())), preferred_element_type=F32
    )


def ones_where(mask):
    return jnp.where(mask, jnp.float32(1), jnp.float32(0)).astype(BF)


def rounded_up(value, unit):
    return -(-value // unit) * unit


def spread_column(row):
    return jnp.transpose(jnp.broadcast_to(row, (LANES, row.shape[1])))


def lane_tiled(column, lanes):
    return jnp.concatenate([column] * (lanes // LANES), axis=1)


def call(kernel, out_shape, args, scratch=(), smem=0, flops=0, limit=40 << 20):
    specs = [pl.BlockSpec(memory_space=pltpu.SMEM)] * smem
    specs += [pl.BlockSpec(memory_space=VM)] * (len(args) - smem)
    return pl.pallas_call(
        kernel,
        out_shape=out_shape,
        in_specs=specs,
        out_specs=jax.tree.map(lambda _: pl.BlockSpec(memory_space=VM), out_shape),
        scratch_shapes=list(scratch),
        compiler_params=pltpu.CompilerParams(vmem_limit_bytes=limit),
        cost_estimate=pl.CostEstimate(
            flops=flops, bytes_accessed=4 << 20, transcendentals=0
        ),
    )(*args)


def shape(dims, kind):
    return jax.ShapeDtypeStruct(dims, kind)


def tiles(total, size):
    size = min(total, size)

    def loop(body):
        def step(i, _):
            body(pl.ds(pl.multiple_of(i * size, size), size), i)
            return 0

        lax.fori_loop(0, total // size, step, 0)

    return loop


def export_kernel(states, export_row, sent):
    rows = states.shape[0]
    slots = export_row.shape[1]
    size = min(256, slots)

    @tiles(slots, size)
    def _(block, i):
        column = lane_tiled(spread_column(export_row[:, block]), rows)
        hot = ones_where(column == lax.broadcasted_iota(jnp.int32, (size, rows), 1))
        sent[block, :] = dot(hot, states[...]).astype(BF)


def setup_kernel(
    slots,
    tile_count,
    src_row,
    dst_row,
    rel_row,
    coef,
    coef_t,
    rel_emb,
    basis,
    states,
    self_weight,
    gate_weight,
    gate_bias,
    mix,
    counts,
    degree_inv,
    partial,
    gate,
    target,
    edge_coef,
    rel_images,
):
    rows, width = states.shape
    edges = src_row.shape[1]
    relations, blocks = coef.shape
    live_edges = tile_count[0, 0] * TILE
    size = 256

    @tiles(edges, size)
    def _(block, i):
        column = lane_tiled(spread_column(dst_row[:, block]), rows)
        edge = lax.broadcasted_iota(jnp.int32, (size, rows), 0) + i * size
        row = lax.broadcasted_iota(jnp.int32, (size, rows), 1)
        target[block, :] = ones_where((column == row) & (edge < live_edges))

    rel_hot = ones_where(
        rel_row[...] == lax.broadcasted_iota(jnp.int32, (relations, edges), 0)
    )
    edge_coef[...] = dot(coef_t[...].astype(BF), rel_hot)
    counts[...] = dot(rel_hot, target[...]).astype(BF)
    degree = 1.0 + dot(jnp.ones((8, edges), BF), target[...])
    degree_inv[...] = spread_column((1.0 / degree)[:1])
    part = min(256, slots)
    for b in range(blocks):

        @tiles(slots, part)
        def _(block, i):
            slot = lax.broadcasted_iota(jnp.int32, (part, edges), 0) + i * part
            weighted = jnp.where(
                src_row[...] == slot,
                jnp.broadcast_to(edge_coef[b : b + 1, :], (part, edges)),
                jnp.float32(0),
            ).astype(BF)
            mix[pl.ds(pl.multiple_of(b * slots + i * part, part), part), :] = dot(
                weighted, target[...]
            ).astype(BF)

    folded = jnp.zeros((relations, width), F32)
    for b in range(blocks):
        folded += coef[:, b : b + 1] * dot(
            rel_emb[...], basis[:, b * width : (b + 1) * width]
        )
    rel_images[...] = folded.astype(BF)

    @tiles(rows, 256)
    def _(block, i):
        own = states[block, :]
        partial[block, :] = dot(own, self_weight[...]) + dot(
            counts[:, block], rel_images[...], 0, 0
        )
        gate[block, :] = lax.logistic(dot(own, gate_weight[...]) + gate_bias[...])


def forward_kernel(
    slots,
    received,
    basis,
    mix,
    degree_inv,
    partial,
    gate,
    states,
    images,
    alpha,
    beta,
):
    rows, width = states.shape
    blocks = basis.shape[1] // width
    part = min(256, slots)
    for b in range(blocks):

        @tiles(slots, part)
        def _(block, i):
            images[pl.ds(pl.multiple_of(b * slots + i * part, part), part), :] = dot(
                received[block, :], basis[:, b * width : (b + 1) * width]
            ).astype(BF)

    @tiles(rows, 256)
    def _(block, i):
        scale = lane_tiled(degree_inv[block, :], width)
        summed = (dot(mix[:, block], images[...], 0, 0) + partial[block, :]) * scale
        aggregated = jnp.tanh(summed)
        opened = gate[block, :]
        alpha[block, :] = opened * (1.0 - aggregated * aggregated) * scale
        beta[block, :] = (
            (aggregated - states[block, :].astype(F32)) * opened * (1.0 - opened)
        )


def upstream_of(block, i, cotangent, handed, handed_slots, export_row):
    total = cotangent[block, :].astype(F32)
    if handed is not None:
        size = total.shape[0]
        slots = export_row.shape[1]
        row = lax.broadcasted_iota(jnp.int32, (size, slots), 0) + i * size
        hot = ones_where(export_row[...] == row)
        total = total + handed[block, :].astype(F32) + dot(hot, handed_slots[...])
    return total


def dense_kernel(first, last, *refs):
    refs = list(refs)
    cotangent, alpha, beta, gate, self_weight, gate_weight = refs[:6]
    refs = refs[6:]
    handed = handed_slots = export_row = None
    if not first:
        handed, handed_slots, export_row = refs[:3]
        refs = refs[3:]
    if last:
        row_grad, dense, gate_row, bias = refs
        bias[...] = jnp.zeros_like(bias)
    else:
        row_grad, dense = refs
    rows = cotangent.shape[0]
    size = 256

    @tiles(rows, size)
    def _(block, i):
        upstream = upstream_of(block, i, cotangent, handed, handed_slots, export_row)
        row_value = (upstream * alpha[block, :]).astype(BF)
        gate_value = upstream * beta[block, :]
        gate_small = gate_value.astype(BF)
        row_grad[block, :] = row_value
        value = (
            upstream * (1.0 - gate[block, :])
            + dot(row_value, self_weight[...], 1, 1)
            + dot(gate_small, gate_weight[...], 1, 1)
        )
        dense[block, :] = value.astype(dense.dtype)
        if last:
            gate_row[block, :] = gate_small
            bias[...] += jnp.sum(gate_value, axis=0, keepdims=True)


def slot_kernel(slots, row_grad, mix, basis, slot_grad, mixed):
    width = row_grad.shape[1]
    blocks = basis.shape[1] // width
    part = min(256, slots)

    @tiles(slots, part)
    def _(block, i):
        total = jnp.zeros((part, width), F32)
        for b in range(blocks):
            at = pl.ds(pl.multiple_of(b * slots + i * part, part), part)
            value = dot(mix[at, :], row_grad[...]).astype(BF)
            mixed[at, :] = value
            total += dot(value, basis[:, b * width : (b + 1) * width], 1, 1)
        slot_grad[block, :] = total.astype(BF)


def weight_kernel(
    slots,
    parts,
    tile_count,
    row_grad,
    gate_row,
    states,
    received,
    mixed,
    counts,
    coef,
    rel_emb,
    basis,
    bias,
    images,
    src_row,
    dst_row,
    rel_row,
    packed,
    scaled,
    edge_grad,
):
    rows, width = states.shape
    relations, blocks = coef.shape
    edges = src_row.shape[1]
    cut = width // parts
    rel_cut = relations // parts
    rel_sum = dot(counts[...], row_grad[...])
    rel_grad = jnp.zeros((relations, width), F32)
    corner = []
    for b in range(blocks):
        columns = slice(b * width, (b + 1) * width)
        value = (coef[:, b : b + 1] * rel_sum).astype(BF)
        scaled[...] = value
        rel_grad += dot(value, basis[:, columns], 1, 1)
        corner.append(
            jnp.sum(
                rel_sum * dot(rel_emb[...], basis[:, columns]), axis=1, keepdims=True
            )
        )
        total = dot(received[...], mixed[b * slots : (b + 1) * slots, :], 0, 0) + dot(
            rel_emb[...], scaled[...], 0, 0
        )
        for p in range(parts):
            packed[p, b * cut : (b + 1) * cut, :] = total[p * cut : (p + 1) * cut].astype(
                BF
            )
    at = blocks * cut
    for grads in (row_grad, gate_row):
        total = dot(states[...], grads[...], 0, 0)
        for p in range(parts):
            packed[p, at : at + cut, :] = total[p * cut : (p + 1) * cut].astype(BF)
        at += cut
    rel_room = rounded_up(rel_cut, 16)
    for p in range(parts):
        value = rel_grad[p * rel_cut : (p + 1) * rel_cut]
        if rel_room > rel_cut:
            value = jnp.concatenate(
                [value, jnp.zeros((rel_room - rel_cut, width), F32)], axis=0
            )
        packed[p, at : at + rel_room, :] = value.astype(BF)
    at += rel_room

    size = 256
    live_edges = tile_count[0, 0] * TILE

    def edge_step(i, sums):
        block = pl.ds(pl.multiple_of(i * size, size), size)
        column = lane_tiled(spread_column(dst_row[:, block]), rows)
        edge = lax.broadcasted_iota(jnp.int32, (size, rows), 0) + i * size
        row = lax.broadcasted_iota(jnp.int32, (size, rows), 1)
        hot = ones_where((column == row) & (edge < live_edges))
        edge_grad[...] = dot(hot, row_grad[...]).astype(BF)
        slot_column = lane_tiled(spread_column(src_row[:, block]), slots)
        own = slot_column == lax.broadcasted_iota(jnp.int32, (size, slots), 1)
        rel_hot = ones_where(
            rel_row[:, block] == lax.broadcasted_iota(jnp.int32, (relations, size), 0)
        )
        out = []
        for b in range(blocks):
            product = dot(edge_grad[...], images[b * slots : (b + 1) * slots, :], 1, 1)
            inner = jnp.sum(
                jnp.where(own, product, jnp.float32(0)), axis=1, keepdims=True
            )
            spread = jnp.broadcast_to(inner, (size, LANES))
            high = spread.astype(BF)
            low = (spread - high.astype(F32)).astype(BF)
            out.append(sums[b] + dot(rel_hot, high) + dot(rel_hot, low))
        return tuple(out)

    sums = lax.fori_loop(
        0,
        edges // size,
        edge_step,
        tuple(jnp.zeros((relations, LANES), F32) for _ in range(blocks)),
    )
    lane = lax.broadcasted_iota(jnp.int32, (relations, LANES), 1)
    gathered = jnp.zeros((relations, LANES), F32)
    for b in range(blocks):
        gathered = jnp.where(lane == b, sums[b] + corner[b], gathered)
    turned = jnp.transpose(gathered)[:8]
    if relations < width:
        turned = jnp.concatenate(
            [turned, jnp.zeros((8, width - relations), F32)], axis=1
        )
    bias8 = jnp.broadcast_to(bias[...], (8, width))
    for p in range(parts):
        rest = packed.shape[1] - at
        lines = [
            turned if p == 0 else pltpu.roll(turned, width - p * rel_cut, 1),
            bias8 if p == 0 else pltpu.roll(bias8, width - p * cut, 1),
        ]
        if rest > 16:
            lines.append(jnp.zeros((rest - 16, width), F32))
        packed[p, at:, :] = jnp.concatenate(lines, axis=0).astype(BF)


def output_kernel(dense, returned, export_row, total):
    rows = dense.shape[0]
    slots = export_row.shape[1]
    size = 256

    @tiles(rows, size)
    def _(block, i):
        row = lax.broadcasted_iota(jnp.int32, (size, slots), 0) + i * size
        hot = ones_where(export_row[...] == row)
        total[block, :] = dense[block, :] + dot(hot, returned[...])


def from_next(block, axis):
    count = lax.axis_size(axis)
    return lax.ppermute(block, axis, [(i, i - 1) for i in range(1, count)])


def halve_over(values, axis):
    count = lax.axis_size(axis)
    index = lax.axis_index(axis)
    distance = 1
    while distance < count:
        left = values.shape[0] // 2
        bit = (index // distance) % 2
        pairs = values.reshape((left, 2) + values.shape[1:])
        sent = lax.dynamic_index_in_dim(pairs, 1 - bit, 1, keepdims=False)
        kept = lax.dynamic_index_in_dim(pairs, bit, 1, keepdims=False)
        route = [(i, i ^ distance) for i in range(count)]
        taken = lax.ppermute(sent, axis, route)
        values = kept.astype(F32) + taken.astype(F32)
        distance *= 2
        if distance < count:
            values = values.astype(BF)
    return values[0]


def per_device(
    states,
    cotangent,
    export_rows,
    edge_src,
    edge_dst,
    edge_rel,
    tile_count,
    basis,
    coef,
    rel_emb,
    self_weight,
    gate_weight,
    gate_bias,
):
    ent_count = lax.axis_size("ent")
    section_count = lax.axis_size("tm")
    own = states[0]
    cot = cotangent[0]
    rows, width = own.shape
    blocks = basis.shape[1] // width
    relations = rel_emb.shape[0]
    edges = edge_src.shape[1]
    slots = export_rows.shape[1]
    per_owner = slots // ent_count

    def exchange(block):
        return lax.all_to_all(
            block.reshape(ent_count, per_owner, width), "ent", 0, 0, tiled=True
        ).reshape(slots, width)

    sent = call(
        export_kernel,
        shape((slots, width), BF),
        (own, export_rows),
        flops=2 * slots * rows * width,
    )
    received = exchange(sent)
    export_next = from_next(export_rows, "tm")
    mix, counts, degree_inv, partial, gate = call(
        functools.partial(setup_kernel, slots),
        (
            shape((blocks * slots, rows), BF),
            shape((relations, rows), BF),
            shape((rows, LANES), F32),
            shape((rows, width), F32),
            shape((rows, width), F32),
        ),
        (
            tile_count,
            edge_src,
            edge_dst,
            edge_rel,
            coef,
            coef.T,
            rel_emb,
            basis,
            own,
            self_weight,
            gate_weight,
            gate_bias[None],
        ),
        scratch=(
            VM((edges, rows), BF),
            VM((blocks, edges), F32),
            VM((relations, width), BF),
        ),
        smem=1,
        flops=2 * blocks * slots * rows * edges,
    )
    images, alpha, beta = call(
        functools.partial(forward_kernel, slots),
        (
            shape((blocks * slots, width), BF),
            shape((rows, width), F32),
            shape((rows, width), F32),
        ),
        (received, basis, mix, degree_inv, partial, gate, own),
        flops=4 * blocks * slots * rows * width,
    )

    handed = None
    for step in range(section_count):
        first, last = step == 0, step + 1 == section_count
        args = (cot, alpha, beta, gate, self_weight, gate_weight)
        if not first:
            args += handed
        outs = (shape((rows, width), BF), shape((rows, width), F32 if last else BF))
        if last:
            outs += (shape((rows, width), BF), shape((1, width), F32))
        outs = call(
            functools.partial(dense_kernel, first, last),
            outs,
            args,
            flops=4 * rows * width * width,
        )
        row_grad, dense = outs[:2]
        slot_grad, mixed = call(
            functools.partial(slot_kernel, slots),
            (shape((slots, width), BF), shape((blocks * slots, width), BF)),
            (row_grad, mix, basis),
            flops=4 * blocks * slots * rows * width,
        )
        if not last:
            ahead = from_next(dense, "tm")
            returned = exchange(slot_grad)
            handed = (ahead, from_next(returned, "tm"), export_next)
    gate_row, bias = outs[2:]

    cut, rel_cut = width // ent_count, relations // ent_count
    rel_room = rounded_up(rel_cut, 16)
    used = (blocks + 2) * cut + rel_room
    depth = rounded_up(used + 16, 16 * section_count)
    packed = call(
        functools.partial(weight_kernel, slots, ent_count),
        shape((ent_count, depth, width), BF),
        (
            tile_count,
            row_grad,
            gate_row,
            own,
            received,
            mixed,
            counts,
            coef,
            rel_emb,
            basis,
            bias,
            images,
            edge_src,
            edge_dst,
            edge_rel,
        ),
        scratch=(VM((relations, width), BF), VM((256, width), BF)),
        smem=1,
        flops=8 * blocks * slots * rows * width,
    )
    returned = exchange(slot_grad)
    state_grad = call(
        output_kernel,
        shape((rows, width), F32),
        (dense, returned, export_rows),
        flops=2 * rows * slots * width,
    )

    own_block = halve_over(packed, "ent").astype(BF)
    quarters = lax.all_to_all(
        own_block.reshape(section_count, depth // section_count, width),
        "tm",
        0,
        0,
        tiled=True,
    )
    quarter = jnp.sum(quarters.astype(F32), axis=0).astype(BF)
    final = lax.all_gather(quarter, "tm", axis=0, tiled=True).astype(F32)
    grad_basis = (
        final[: blocks * cut].reshape(blocks, cut, width).transpose(1, 0, 2)
    ).reshape(cut, blocks * width)
    at = blocks * cut
    grad_self = final[at : at + cut]
    grad_gate = final[at + cut : at + 2 * cut]
    at += 2 * cut
    grad_rel = final[at : at + rel_cut]
    at += rel_room
    grad_coef = final[at : at + blocks, :rel_cut].T
    grad_bias = final[at + 8, :cut]
    return state_grad[None], grad_basis, grad_self, grad_gate, grad_bias, grad_coef, grad_rel


def solution(mesh):
    placed = (P("tm", "ent", None),) * 2 + (P("tm", "ent"),) * 5 + (P(),) * 6
    return jax.shard_map(
        per_device,
        mesh=mesh,
        in_specs=placed,
        out_specs=(
            P("tm", "ent", None),
            P("ent", None),
            P("ent", None),
            P("ent", None),
            P("ent"),
            P("ent", None),
            P("ent", None),
        ),
        check_vma=False,
    )
```

time: 502 us -> 259 us (0.52)
  other arithmetic: 101 us -> 6.08 us
  matrix products: 87.5 us -> 0 us
  waiting for transfers between devices: 168 us -> 91.8 us
  Pallas kernels: 0 us -> 48.1 us
  local copies, waits for them, and re-layouts: 56.4 us -> 38.5 us
  between operations: 15.7 us -> 1.76 us
  blocking collectives: 41.7 us -> 47.3 us
    psum x1 -> x0, waiting for transfers between devices: 89.6 us -> none  [per_device(): lax.psum((basis_term, self_term, gate_term, bias_term, coef_term, relatio...]
    dot_general x24 -> x0, matrix products: 87.5 us -> none  [the longest x4 24.7 us: per_device(): lax.dot_general(gate_row, gate_weight, contract_last, preferred_element_t...]
    scatter-add x10 -> x0, other arithmetic: 74.1 us -> none  [the longest x4 32.6 us: per_device(): slot_grad = jax.ops.segment_sum(input_grad, edge_source, slot_count)]
    pallas_call x0 -> x13, Pallas kernels: none -> 48.1 us  [call(): pl.pallas_call(kernel, out_shape=out_shape, in_specs=specs, out_specs=jax...]
    psum x1 -> x0, blocking collectives: 41.7 us -> none  [per_device(): lax.psum((basis_term, self_term, gate_term, bias_term, coef_term, relatio...]
    all_to_all x0 -> x3, blocking collectives: none -> 31.8 us  [exchange(): lax.all_to_all(block.reshape(ent_count, per_owner, width), 'ent', 0, 0, t...]
    gather x6 -> x0, local copies, waits for them, and re-layouts: 27.6 us -> none  [the longest x4 20.3 us: per_device(): row_grad[edge_target]]
    unnamed x80 -> x97, local copies, waits for them, and re-layouts: 12 us -> 34.2 us
  transfers between devices with their start and end apart: 9 -> 13, of which waited for: 7 -> 7; matrix products, arithmetic and copies ran while one was open for 13% -> 1% of each run, Pallas kernels for 0% -> 7%
where the time goes in v1:
time: 259 us; the launch traced here: 257 us
  waiting for transfers between devices  91.8 us (35%)
  Pallas kernels  48.1 us (19%)
  blocking collectives  47.3 us (18%)
  local copies, waits for them, and re-layouts  38.5 us (15%)
  starting transfers between devices  23.6 us (9%)
  other arithmetic  6.08 us (2%)
    pallas_call x13, Pallas kernels, call(): pl.pallas_call(kernel, out_shape=out_shape, in_specs=specs, out_specs=jax...  48.1 us
    ppermute x7, waiting for transfers between devices, from_next(): return lax.ppermute(block, axis, [(i, i - 1) for i in range(1, count)])  47.3 us
    ppermute x3, waiting for transfers between devices, halve_over(): taken = lax.ppermute(sent, axis, route)  35.3 us
    unnamed x97, local copies, waits for them, and re-layouts  34.2 us
    all_to_all x3, blocking collectives, exchange(): lax.all_to_all(block.reshape(ent_count, per_owner, width), 'ent', 0, 0, t...  31.8 us
    all_gather x1, blocking collectives, per_device(): final = lax.all_gather(quarter, 'tm', axis=0, tiled=True).astype(F32)  15.5 us
    ppermute x7, starting transfers between devices, from_next(): return lax.ppermute(block, axis, [(i, i - 1) for i in range(1, count)])  9.26 us
    all_to_all x1, waiting for transfers between devices, per_device(): lax.all_to_all(own_block.reshape(section_count, depth // section_count, w...  9.22 us
  transfers between devices with their start and end apart: 13, of which 7 were waited for; matrix products, arithmetic and copies ran while one was open for 1% of the time, Pallas kernels for 7%

profile of v1, /device:TPU:0, one launch (start us, length us, event | category | flops | bytes accessed | tf_op | source)
XLA Modules:
  0.0 257.2 jit_solution(3480166215431656630)
XLA Ops:
  3.8 5.2 %all-to-all-start = ((bf16[8,32,512]{2,1,0:T(8,128)(2,1)}), bf16[8,32,512]{2,1,0:T(8,128)(2,1)S(1)}, u32[]{:S(2)}, u32[]{:S(2)}) async-start(bf16[8,32,512]{2,1,0:T(8,128)(2,1)} %bitcast.2), calls=%async_computation | async-start | bytes 524288 | tf_op jit(solution)/shard_map/all_to_all | solution.py:435
  19.7 6.7 %shard_map.181 = (bf16[1024,1024]{1,0:T(8,128)(2,1)S(1)}, bf16[256,1024]{1,0:T(8,128)(2,1)S(1)}, f32[1024,128]{1,0:T(8,128)S(1)}, f32[1024,512]{1,0:T(8,128)S(1)}, f32[1024,512]{1,0:T(8,128)S(1)}) custom-call(s32[1,1]{1,0:T(1,128)S(6)} %copy.24.tile_count, s32[1,1024]{1,0:T(1,128)S(1)} %copy-done.39, s32[1,1024]{1,0:T(1,128)S(1)} %copy-done.41, ...), custom_call_target="tpu_custom_call" | custom-call | flops 2147483648 | bytes 4194304 | tf_op jit(solution)/shard_map/pallas_call | solution.py:42
  39.1 5.0 %shard_map.182 = (bf16[1024,512]{1,0:T(8,128)(2,1)S(1)}, f32[1024,512]{1,0:T(8,128)S(1)}, f32[1024,512]{1,0:T(8,128)S(1)}) custom-call(bf16[256,512]{1,0:T(8,128)(2,1)S(1)} %bitcast.47, bf16[512,2048]{1,0:T(8,128)(2,1)S(1)} %copy-done.19, bf16[1024,1024]{1,0:T(8,128)(2,1)S(1)} %copy-done.23, f32[1024,128]{1,0:T(8,128)S(1)} %copy-done.31, ...), custom_call_target="tpu_custom_call" | custom-call | flops 2147483648 | bytes 4194304 | tf_op jit(solution)/shard_map/pallas_call | solution.py:42
  48.5 2.9 %shard_map.184 = (bf16[256,512]{1,0:T(8,128)(2,1)S(1)}, bf16[1024,512]{1,0:T(8,128)(2,1)}) custom-call(bf16[1024,512]{1,0:T(8,128)(2,1)S(1)} %get-tuple-element.37.row_grad, bf16[1024,1024]{1,0:T(8,128)(2,1)S(1)} %copy-done.23, bf16[512,2048]{1,0:T(8,128)(2,1)S(1)} %copy-done.20), custom_call_target="tpu_custom_call" | custom-call | flops 2147483648 | bytes 4194304 | tf_op jit(solution)/shard_map/pallas_call | solution.py:42
  51.4 10.9 %all_to_all.30 = bf16[8,32,512]{2,1,0:T(8,128)(2,1)S(1)} all-to-all(bf16[8,32,512]{2,1,0:T(8,128)(2,1)S(1)} %bitcast.50), channel_id=1, replica_groups=mesh['tm'=4,'ent'=8] {'ent'}, dimensions={0} | all-to-all | bytes 524288 | tf_op jit(solution)/shard_map/all_to_all | solution.py:435
  65.0 15.3 %collective-permute-done.2.refs_8_ = s32[1,256]{1,0:T(1,128)S(1)} collective-permute-done((s32[1,256]{1,0:T(1,128)S(1)}, s32[1,256]{1,0:T(1,128)S(1)}, u32[]{:S(2)}, u32[]{:S(2)}) %collective-permute-start.2) | collective-permute-done | bytes 1056 | tf_op jit(solution)/shard_map/ppermute | solution.py:386
  84.0 2.9 %shard_map.186 = (bf16[256,512]{1,0:T(8,128)(2,1)S(1)}, bf16[1024,512]{1,0:T(8,128)(2,1)}) custom-call(bf16[1024,512]{1,0:T(8,128)(2,1)S(1)} %get-tuple-element.40.row_grad, bf16[1024,1024]{1,0:T(8,128)(2,1)S(1)} %copy-done.24, bf16[512,2048]{1,0:T(8,128)(2,1)S(1)} %copy-done.20), custom_call_target="tpu_custom_call" | custom-call | flops 2147483648 | bytes 4194304 | tf_op jit(solution)/shard_map/pallas_call | solution.py:42
  86.9 10.5 %all_to_all.31 = bf16[8,32,512]{2,1,0:T(8,128)(2,1)S(1)} all-to-all(bf16[8,32,512]{2,1,0:T(8,128)(2,1)S(1)} %bitcast.51), channel_id=1, replica_groups=mesh['tm'=4,'ent'=8] {'ent'}, dimensions={0} | all-to-all | bytes 524288 | tf_op jit(solution)/shard_map/all_to_all | solution.py:435
  98.7 16.2 %collective-permute-done.4.refs_7_ = bf16[256,512]{1,0:T(8,128)(2,1)S(1)} collective-permute-done((bf16[256,512]{1,0:T(8,128)(2,1)S(1)}, bf16[256,512]{1,0:T(8,128)(2,1)S(1)}, u32[]{:S(2)}, u32[]{:S(2)}) %collective-permute-start.4) | collective-permute-done | bytes 262176 | tf_op jit(solution)/shard_map/ppermute | solution.py:386
  114.9 3.3 %shard_map.187 = (bf16[1024,512]{1,0:T(8,128)(2,1)S(1)}, bf16[1024,512]{1,0:T(8,128)(2,1)}) custom-call(bf16[1024,512]{1,0:T(8,128)(2,1)S(1)} %bitcast.39, f32[1024,512]{1,0:T(8,128)S(1)} %get-tuple-element.34.refs_1_, f32[1024,512]{1,0:T(8,128)S(1)} %get-tuple-element.35.refs_2_, f32[1024,512]{1,0:T(8,128)S(1)} %copy-done.1, ...), custom_call_target="tpu_custom_call" | custom-call | flops 1073741824 | bytes 4194304 | tf_op jit(solution)/shard_map/pallas_call | solution.py:42
  119.5 2.9 %shard_map.188 = (bf16[256,512]{1,0:T(8,128)(2,1)S(1)}, bf16[1024,512]{1,0:T(8,128)(2,1)}) custom-call(bf16[1024,512]{1,0:T(8,128)(2,1)S(1)} %get-tuple-element.43.row_grad, bf16[1024,1024]{1,0:T(8,128)(2,1)S(1)} %copy-done.24, bf16[512,2048]{1,0:T(8,128)(2,1)S(1)} %copy-done.20), custom_call_target="tpu_custom_call" | custom-call | flops 2147483648 | bytes 4194304 | tf_op jit(solution)/shard_map/pallas_call | solution.py:42
  122.4 10.4 %all_to_all.32 = bf16[8,32,512]{2,1,0:T(8,128)(2,1)} all-to-all(bf16[8,32,512]{2,1,0:T(8,128)(2,1)S(1)} %bitcast.52), channel_id=1, replica_groups=mesh['tm'=4,'ent'=8] {'ent'}, dimensions={0} | all-to-all | bytes 524288 | tf_op jit(solution)/shard_map/all_to_all | solution.py:435
  134.1 15.7 %collective-permute-done.6.refs_7_ = bf16[256,512]{1,0:T(8,128)(2,1)} collective-permute-done((bf16[256,512]{1,0:T(8,128)(2,1)}, bf16[256,512]{1,0:T(8,128)(2,1)}, u32[]{:S(2)}, u32[]{:S(2)}) %collective-permute-start.6) | collective-permute-done | bytes 262176 | tf_op jit(solution)/shard_map/ppermute | solution.py:386
  155.1 4.2 %shard_map.189 = (bf16[1024,512]{1,0:T(8,128)(2,1)S(1)}, f32[1024,512]{1,0:T(8,128)S(1)}, bf16[1024,512]{1,0:T(8,128)(2,1)S(1)}, f32[1,512]{1,0:T(1,128)S(1)}) custom-call(bf16[1024,512]{1,0:T(8,128)(2,1)S(1)} %bitcast.40, f32[1024,512]{1,0:T(8,128)S(1)} %copy-done.3, f32[1024,512]{1,0:T(8,128)S(1)} %copy-done.5, f32[1024,512]{1,0:T(8,128)S(1)} %copy-done.1, ...), custom_call_target="tpu_custom_call" | custom-call | flops 1073741824 | bytes 4194304 | tf_op jit(solution)/shard_map/pallas_call | solution.py:42
  160.7 2.7 %shard_map.190 = (bf16[256,512]{1,0:T(8,128)(2,1)}, bf16[1024,512]{1,0:T(8,128)(2,1)S(1)}) custom-call(bf16[1024,512]{1,0:T(8,128)(2,1)S(1)} %get-tuple-element.46.row_grad, bf16[1024,1024]{1,0:T(8,128)(2,1)S(1)} %copy-done.25, bf16[512,2048]{1,0:T(8,128)(2,1)S(1)} %copy-done.21), custom_call_target="tpu_custom_call" | custom-call | flops 2147483648 | bytes 4194304 | tf_op jit(solution)/shard_map/pallas_call | solution.py:42
  163.5 9.9 %shard_map.192 = bf16[8,448,512]{2,1,0:T(8,128)(2,1)S(1)} custom-call(s32[1,1]{1,0:T(1,128)S(6)} %copy.24.tile_count, bf16[1024,512]{1,0:T(8,128)(2,1)S(1)} %get-tuple-element.46.row_grad, bf16[1024,512]{1,0:T(8,128)(2,1)S(1)} %get-tuple-element.48.gate_row, bf16[1024,512]{1,0:T(8,128)(2,1)S(1)} %bitcast.44, bf16[256,512]{1,0:T(8,128)(2,1)S(1)} %bitcast.48, ...), custom_call_target="tpu_custom_call" | custom-call | flops 4294967296 | bytes 4194304 | tf_op jit(solution)/shard_map/pallas_call | solution.py:42
  175.5 3.9 %collective-permute-done.7 = bf16[4,448,512]{2,1,0:T(8,128)(2,1)} collective-permute-done((bf16[4,448,512]{2,1,0:T(8,128)(2,1)S(1)}, bf16[4,448,512]{2,1,0:T(8,128)(2,1)}, u32[]{:S(2)}, u32[]{:S(2)}) %collective-permute-start.7) | collective-permute-done | bytes 1835040 | tf_op jit(solution)/shard_map/ppermute | solution.py:400
  179.3 2.6 fusion
  182.9 21.7 %collective-permute-done.8 = bf16[2,448,512]{2,1,0:T(8,128)(2,1)} collective-permute-done((bf16[2,448,512]{2,1,0:T(8,128)(2,1)S(1)}, bf16[2,448,512]{2,1,0:T(8,128)(2,1)}, u32[]{:S(2)}, u32[]{:S(2)}) %collective-permute-start.8) | collective-permute-done | bytes 917536 | tf_op jit(solution)/shard_map/ppermute | solution.py:400
  207.7 3.4 %all-to-all-start.4 = ((bf16[8,32,512]{2,1,0:T(8,128)(2,1)}), bf16[8,32,512]{2,1,0:T(8,128)(2,1)S(1)}, u32[]{:S(2)}, u32[]{:S(2)}) async-start(bf16[8,32,512]{2,1,0:T(8,128)(2,1)} %bitcast.12), calls=%async_computation.4 | async-start | bytes 524288 | tf_op jit(solution)/shard_map/all_to_all | solution.py:435
  211.1 9.8 %collective-permute-done.9 = bf16[1,448,512]{2,1,0:T(8,128)(2,1)} collective-permute-done((bf16[1,448,512]{2,1,0:T(8,128)(2,1)}, bf16[1,448,512]{2,1,0:T(8,128)(2,1)}, u32[]{:S(2)}, u32[]{:S(2)}) %collective-permute-start.9) | collective-permute-done | bytes 458784 | tf_op jit(solution)/shard_map/ppermute | solution.py:400
  222.8 3.9 %all-to-all-start.5 = ((bf16[4,112,512]{2,1,0:T(8,128)(2,1)}), bf16[4,112,512]{2,1,0:T(8,128)(2,1)S(1)}, u32[]{:S(2)}, u32[]{:S(2)}) async-start(bf16[4,112,512]{2,1,0:T(8,128)(2,1)} %bitcast.59), calls=%async_computation.5 | async-start | bytes 917504 | tf_op jit(solution)/shard_map/all_to_all | solution.py:554
  228.9 9.2 %all-to-all-done.5 = bf16[4,112,512]{2,1,0:T(8,128)(2,1)S(1)} async-done(((bf16[4,112,512]{2,1,0:T(8,128)(2,1)}), bf16[4,112,512]{2,1,0:T(8,128)(2,1)S(1)}, u32[]{:S(2)}, u32[]{:S(2)}) %all-to-all-start.5) | async-done | bytes 458784 | tf_op jit(solution)/shard_map/all_to_all | solution.py:554
  238.2 15.5 %all_gather.3 = bf16[448,512]{1,0:T(8,128)(2,1)S(1)} all-gather(bf16[112,512]{1,0:T(8,128)(2,1)S(1)} %reduce_sum.12), channel_id=1, replica_groups=mesh['tm'=4,'ent'=8] {'tm'}, dimensions={0}, use_global_device_ids=true | all-gather | bytes 573440 | tf_op jit(solution)/shard_map/all_gather | solution.py:562
  (130 shorter events, 60.9 us)
Async XLA Ops:
  3.8 28.2 %all-to-all-start = ((bf16[8,32,512]{2,1,0:T(8,128)(2,1)}), bf16[8,32,512]{2,1,0:T(8,128)(2,1)S(1)}, u32[]{:S(2)}, u32[]{:S(2)}) async-start(bf16[8,32,512]{2,1,0:T(8,128)(2,1)} %bitcast.2), calls=%async_computation | async-start | bytes 524288 | tf_op jit(solution)/shard_map/all_to_all | solution.py:435
  39.0 6.0 %copy-start.1 = (f32[1024,512]{1,0:T(8,128)S(1)}, f32[1024,512]{1,0:T(8,128)}, u32[]{:S(2)}) copy-start(f32[1024,512]{1,0:T(8,128)} %copy-done) | copy-start | bytes 6291460
  39.0 6.0 %copy-start.6 = (bf16[1,1024,512]{2,1,0:T(8,128)(2,1)S(1)}, bf16[1,1024,512]{2,1,0:T(8,128)(2,1)}, u32[]{:S(2)}) copy-start(bf16[1,1024,512]{2,1,0:T(8,128)(2,1)} %param.14) | copy-start | bytes 3145732
  39.0 6.0 %copy-start.8 = (bf16[512,512]{1,0:T(8,128)(2,1)S(1)}, bf16[512,512]{1,0:T(8,128)(2,1)}, u32[]{:S(2)}) copy-start(bf16[512,512]{1,0:T(8,128)(2,1)} %refs_4_.7) | copy-start | bytes 1572868
  39.0 6.1 %copy-start.11 = (bf16[512,512]{1,0:T(8,128)(2,1)S(1)}, bf16[512,512]{1,0:T(8,128)(2,1)}, u32[]{:S(2)}) copy-start(bf16[512,512]{1,0:T(8,128)(2,1)} %refs_5_.7) | copy-start | bytes 1572868
  45.1 69.8 %copy-start.2 = (f32[1024,512]{1,0:T(8,128)}, f32[1024,512]{1,0:T(8,128)S(1)}, u32[]{:S(2)}) copy-start(f32[1024,512]{1,0:T(8,128)S(1)} %get-tuple-element.34.refs_1_) | copy-start | bytes 6291460
  45.1 69.8 %copy-start.4 = (f32[1024,512]{1,0:T(8,128)}, f32[1024,512]{1,0:T(8,128)S(1)}, u32[]{:S(2)}) copy-start(f32[1024,512]{1,0:T(8,128)S(1)} %get-tuple-element.35.refs_2_) | copy-start | bytes 6291460
  47.1 33.3 %collective-permute-start = (bf16[1024,512]{1,0:T(8,128)(2,1)S(1)}, bf16[1024,512]{1,0:T(8,128)(2,1)S(1)}, u32[]{:S(2)}, u32[]{:S(2)}) collective-permute-start(bf16[1024,512]{1,0:T(8,128)(2,1)S(1)} %get-tuple-element.36), channel_id=1, source_target_pairs={{8,0},{16,8},{24,16},{9,1},{17,9},{25,17},{10,2},{18,10},{26,18},{... | collective-permute-start | bytes 3145736 | tf_op jit(solution)/shard_map/ppermute | solution.py:386
  48.5 15.2 %copy-start.34 = (s32[1,256]{1,0:T(1,128)S(1)}, s32[1,256]{1,0:T(1,128)}, u32[]{:S(2)}) copy-start(s32[1,256]{1,0:T(1,128)} %export_row.3) | copy-start | bytes 3076
  62.3 21.7 %copy-start.24 = (bf16[1024,1024]{1,0:T(8,128)(2,1)S(1)}, bf16[1024,1024]{1,0:T(8,128)(2,1)}, u32[]{:S(2)}) copy-start(bf16[1024,1024]{1,0:T(8,128)(2,1)} %copy-done.22) | copy-start | bytes 6291460
  62.3 18.1 %collective-permute-start.1 = (bf16[256,512]{1,0:T(8,128)(2,1)S(1)}, bf16[256,512]{1,0:T(8,128)(2,1)S(1)}, u32[]{:S(2)}, u32[]{:S(2)}) collective-permute-start(bf16[256,512]{1,0:T(8,128)(2,1)S(1)} %bitcast.61), channel_id=1, source_target_pairs={{8,0},{16,8},{24,16},{9,1},{17,9},{25,17},{10,2},{18,10},{26,18},{... | collective-permute-start | bytes 786440 | tf_op jit(solution)/shard_map/ppermute | solution.py:386
  63.7 16.6 %collective-permute-start.2 = (s32[1,256]{1,0:T(1,128)S(1)}, s32[1,256]{1,0:T(1,128)S(1)}, u32[]{:S(2)}, u32[]{:S(2)}) collective-permute-start(s32[1,256]{1,0:T(1,128)S(1)} %copy-done.34), channel_id=1, source_target_pairs={{8,0},{16,8},{24,16},{9,1},{17,9},{25,17},{10,2},{18,10},{26,18},{... | collective-permute-start | bytes 3080 | tf_op jit(solution)/shard_map/ppermute | solution.py:386
  82.7 32.2 %collective-permute-start.3 = (bf16[1024,512]{1,0:T(8,128)(2,1)S(1)}, bf16[1024,512]{1,0:T(8,128)(2,1)S(1)}, u32[]{:S(2)}, u32[]{:S(2)}) collective-permute-start(bf16[1024,512]{1,0:T(8,128)(2,1)S(1)} %get-tuple-element.39), channel_id=1, source_target_pairs={{8,0},{16,8},{24,16},{9,1},{17,9},{25,17},{10,2},{18,10},{26,18},{... | collective-permute-start | bytes 3145736 | tf_op jit(solution)/shard_map/ppermute | solution.py:386
  97.4 17.5 %collective-permute-start.4 = (bf16[256,512]{1,0:T(8,128)(2,1)S(1)}, bf16[256,512]{1,0:T(8,128)(2,1)S(1)}, u32[]{:S(2)}, u32[]{:S(2)}) collective-permute-start(bf16[256,512]{1,0:T(8,128)(2,1)S(1)} %bitcast.62), channel_id=1, source_target_pairs={{8,0},{16,8},{24,16},{9,1},{17,9},{25,17},{10,2},{18,10},{26,18},{... | collective-permute-start | bytes 786440 | tf_op jit(solution)/shard_map/ppermute | solution.py:386
  118.2 31.6 %collective-permute-start.5 = (bf16[1024,512]{1,0:T(8,128)(2,1)}, bf16[1024,512]{1,0:T(8,128)(2,1)}, u32[]{:S(2)}, u32[]{:S(2)}) collective-permute-start(bf16[1024,512]{1,0:T(8,128)(2,1)} %get-tuple-element.42), channel_id=1, source_target_pairs={{8,0},{16,8},{24,16},{9,1},{17,9},{25,17},{10,2},{18,10},{26,18},{... | collective-permute-start | bytes 3145736 | tf_op jit(solution)/shard_map/ppermute | solution.py:386
  132.8 17.0 %collective-permute-start.6 = (bf16[256,512]{1,0:T(8,128)(2,1)}, bf16[256,512]{1,0:T(8,128)(2,1)}, u32[]{:S(2)}, u32[]{:S(2)}) collective-permute-start(bf16[256,512]{1,0:T(8,128)(2,1)} %bitcast.11), channel_id=1, source_target_pairs={{8,0},{16,8},{24,16},{9,1},{17,9},{25,17},{10,2},{18,10},{26,18},{... | collective-permute-start | bytes 786440 | tf_op jit(solution)/shard_map/ppermute | solution.py:386
  155.1 5.5 %copy-start.21 = (bf16[512,2048]{1,0:T(8,128)(2,1)S(1)}, bf16[512,2048]{1,0:T(8,128)(2,1)}, u32[]{:S(2)}) copy-start(bf16[512,2048]{1,0:T(8,128)(2,1)} %basis.13) | copy-start | bytes 6291460
  155.1 5.5 %copy-start.25 = (bf16[1024,1024]{1,0:T(8,128)(2,1)S(1)}, bf16[1024,1024]{1,0:T(8,128)(2,1)}, u32[]{:S(2)}) copy-start(bf16[1024,1024]{1,0:T(8,128)(2,1)} %copy-done.22) | copy-start | bytes 6291460
  175.3 4.0 %collective-permute-start.7 = (bf16[4,448,512]{2,1,0:T(8,128)(2,1)S(1)}, bf16[4,448,512]{2,1,0:T(8,128)(2,1)}, u32[]{:S(2)}, u32[]{:S(2)}) collective-permute-start(bf16[4,448,512]{2,1,0:T(8,128)(2,1)S(1)} %dynamic-slice_bitcast_fusion), channel_id=1, source_target_pairs={{0,1},{1,0},{2,3},{3,2},{4,5},{5,4},{6,7},{7,6},{8,9},{9,8},{10,11... | collective-permute-start | bytes 5505032 | tf_op jit(solution)/shard_map/ppermute | solution.py:400
  182.0 22.6 %collective-permute-start.8 = (bf16[2,448,512]{2,1,0:T(8,128)(2,1)S(1)}, bf16[2,448,512]{2,1,0:T(8,128)(2,1)}, u32[]{:S(2)}, u32[]{:S(2)}) collective-permute-start(bf16[2,448,512]{2,1,0:T(8,128)(2,1)S(1)} %dynamic-slice_bitcast_fusion.1), channel_id=1, source_target_pairs={{0,2},{1,3},{2,0},{3,1},{4,6},{5,7},{6,4},{7,5},{8,10},{9,11},{10,... | collective-permute-start | bytes 2752520 | tf_op jit(solution)/shard_map/ppermute | solution.py:400
  206.0 20.7 %copy-start.29 = (f32[1024,512]{1,0:T(8,128)S(1)}, f32[1024,512]{1,0:T(8,128)}, u32[]{:S(2)}) copy-start(f32[1024,512]{1,0:T(8,128)} %copy-done.28) | copy-start | bytes 6291460
  206.8 14.1 %collective-permute-start.9 = (bf16[1,448,512]{2,1,0:T(8,128)(2,1)}, bf16[1,448,512]{2,1,0:T(8,128)(2,1)}, u32[]{:S(2)}, u32[]{:S(2)}) collective-permute-start(bf16[1,448,512]{2,1,0:T(8,128)(2,1)} %constant_dynamic-slice_fusion), channel_id=1, source_target_pairs={{0,4},{1,5},{2,6},{3,7},{4,0},{5,1},{6,2},{7,3},{8,12},{9,13},{10,... | collective-permute-start | bytes 1376264 | tf_op jit(solution)/shard_map/ppermute | solution.py:400
  207.7 15.1 %all-to-all-start.4 = ((bf16[8,32,512]{2,1,0:T(8,128)(2,1)}), bf16[8,32,512]{2,1,0:T(8,128)(2,1)S(1)}, u32[]{:S(2)}, u32[]{:S(2)}) async-start(bf16[8,32,512]{2,1,0:T(8,128)(2,1)} %bitcast.12), calls=%async_computation.4 | async-start | bytes 524288 | tf_op jit(solution)/shard_map/all_to_all | solution.py:435
  222.8 15.3 %all-to-all-start.5 = ((bf16[4,112,512]{2,1,0:T(8,128)(2,1)}), bf16[4,112,512]{2,1,0:T(8,128)(2,1)S(1)}, u32[]{:S(2)}, u32[]{:S(2)}) async-start(bf16[4,112,512]{2,1,0:T(8,128)(2,1)} %bitcast.59), calls=%async_computation.5 | async-start | bytes 917504 | tf_op jit(solution)/shard_map/all_to_all | solution.py:554
  (37 other events, 56.3 us)

commit v2 on v1

v2 whole, which is shorter than its diff:
```python
import functools

import jax
import jax.numpy as jnp
from jax import lax
from jax.experimental import pallas as pl
from jax.experimental.pallas import tpu as pltpu
from jax.sharding import PartitionSpec as P

TILE = 128
LANES = 128
BF = jnp.bfloat16
F32 = jnp.float32
VM = pltpu.VMEM


def dot(left, right, left_dim=1, right_dim=0):
    return lax.dot_general(
        left, right, (((left_dim,), (right_dim,)), ((), ())), preferred_element_type=F32
    )


def ones_where(mask):
    return jnp.where(mask, jnp.float32(1), jnp.float32(0)).astype(BF)


def rounded_up(value, unit):
    return -(-value // unit) * unit


def spread_column(row):
    return jnp.transpose(jnp.broadcast_to(row, (LANES, row.shape[1])))


def lane_tiled(column, lanes):
    return jnp.concatenate([column] * (lanes // LANES), axis=1)


ANY = pltpu.HBM
FULL = 63 << 20


def call(kernel, outs, args, scratch=(), flops=0, limit=12 << 20):
    single = not isinstance(outs, list)
    listed = [outs] if single else outs
    out_shape = tuple(shape(dims, kind) for dims, kind, _ in listed)
    out_specs = tuple(pl.BlockSpec(memory_space=place) for _, _, place in listed)
    return pl.pallas_call(
        kernel,
        out_shape=out_shape[0] if single else out_shape,
        in_specs=[pl.BlockSpec(memory_space=place) for _, place in args],
        out_specs=out_specs[0] if single else out_specs,
        scratch_shapes=list(scratch),
        compiler_params=pltpu.CompilerParams(vmem_limit_bytes=limit),
        cost_estimate=pl.CostEstimate(
            flops=flops, bytes_accessed=4 << 20, transcendentals=0
        ),
    )(*[array for array, _ in args])


def fetched(sources, places, sems, start=0):
    copies = []
    for k, (source, place) in enumerate(zip(sources, places)):
        copy = pltpu.make_async_copy(source, place, sems.at[start + k])
        copy.start()
        copies.append(copy)
    return copies


def shape(dims, kind):
    return jax.ShapeDtypeStruct(dims, kind)


def tiles(total, size):
    size = min(total, size)

    def loop(body):
        def step(i, _):
            body(pl.ds(pl.multiple_of(i * size, size), size), i)
            return 0

        lax.fori_loop(0, total // size, step, 0)

    return loop


def export_kernel(states_any, export_any, sent_any, states, export_row, sent, sems):
    rows = states.shape[0]
    slots = export_row.shape[1]
    size = min(256, slots)
    copies = fetched((states_any, export_any), (states, export_row), sems)
    copies[1].wait()
    copies[0].wait()

    @tiles(slots, size)
    def _(block, i):
        column = lane_tiled(spread_column(export_row[:, block]), rows)
        hot = ones_where(column == lax.broadcasted_iota(jnp.int32, (size, rows), 1))
        sent[block, :] = dot(hot, states[...]).astype(BF)

    store = pltpu.make_async_copy(sent, sent_any, sems.at[2])
    store.start()
    store.wait()


def setup_kernel(slots, *refs):
    tile_count = refs[0]
    sources = refs[1:11]
    outs = refs[11:16]
    places = refs[16:26]
    results = refs[26:31]
    target, edge_coef, rel_images, in_sems, out_sems = refs[31:]
    dst_row, rel_row, src_row, coef_t, rel_emb, basis = places[:6]
    states, self_weight, gate_weight, gate_bias = places[6:]
    mix, counts, degree_inv, partial, gate = results
    rows, width = states.shape
    edges = src_row.shape[1]
    blocks, relations = coef_t.shape
    live_edges = tile_count[0, 0] * TILE
    size = 256
    copies = fetched(sources, places, in_sems)
    copies[0].wait()

    @tiles(edges, size)
    def _(block, i):
        column = lane_tiled(spread_column(dst_row[:, block]), rows)
        edge = lax.broadcasted_iota(jnp.int32, (size, rows), 0) + i * size
        row = lax.broadcasted_iota(jnp.int32, (size, rows), 1)
        target[block, :] = ones_where((column == row) & (edge < live_edges))

    copies[1].wait()
    rel_hot = ones_where(
        rel_row[...] == lax.broadcasted_iota(jnp.int32, (relations, edges), 0)
    )
    copies[3].wait()
    edge_coef[...] = dot(coef_t[...].astype(BF), rel_hot)
    counts[...] = dot(rel_hot, target[...]).astype(BF)
    degree = 1.0 + dot(jnp.ones((8, edges), BF), target[...])
    degree_inv[...] = spread_column((1.0 / degree)[:1])
    stores = fetched((counts, degree_inv), outs[1:3], out_sems, 0)
    copies[2].wait()
    part = min(256, slots)
    for b in range(blocks):

        @tiles(slots, part)
        def _(block, i):
            slot = lax.broadcasted_iota(jnp.int32, (part, edges), 0) + i * part
            weighted = jnp.where(
                src_row[...] == slot,
                jnp.broadcast_to(edge_coef[b : b + 1, :], (part, edges)),
                jnp.float32(0),
            ).astype(BF)
            mix[pl.ds(pl.multiple_of(b * slots + i * part, part), part), :] = dot(
                weighted, target[...]
            ).astype(BF)

    stores += fetched((mix,), outs[:1], out_sems, 2)
    copies[4].wait()
    copies[5].wait()
    folded = jnp.zeros((relations, width), F32)
    for b in range(blocks):
        scale = lane_tiled(spread_column(coef_t[b : b + 1, :]), width)
        folded += scale * dot(rel_emb[...], basis[:, b * width : (b + 1) * width])
    rel_images[...] = folded.astype(BF)
    for copy in copies[6:]:
        copy.wait()

    @tiles(rows, 256)
    def _(block, i):
        own = states[block, :]
        partial[block, :] = dot(own, self_weight[...]) + dot(
            counts[:, block], rel_images[...], 0, 0
        )
        gate[block, :] = lax.logistic(dot(own, gate_weight[...]) + gate_bias[...])

    stores += fetched((partial, gate), outs[3:], out_sems, 3)
    for copy in stores:
        copy.wait()


def forward_kernel(slots, *refs):
    received = refs[0]
    sources = refs[1:10]
    basis, mix, gate, self_weight, gate_weight, cotangent = refs[10:16]
    alpha, beta, row_grad, dense, images_any = refs[16:21]
    partial, degree_inv, states, images, sems = refs[21:]
    places = (
        basis,
        mix,
        degree_inv,
        partial,
        gate,
        states,
        cotangent,
        self_weight,
        gate_weight,
    )
    rows, width = states.shape
    blocks = basis.shape[1] // width
    part = min(256, slots)
    copies = fetched(sources, places, sems)
    copies[0].wait()
    for b in range(blocks):

        @tiles(slots, part)
        def _(block, i):
            images[pl.ds(pl.multiple_of(b * slots + i * part, part), part), :] = dot(
                received[block, :], basis[:, b * width : (b + 1) * width]
            ).astype(BF)

    store = pltpu.make_async_copy(images, images_any, sems.at[9])
    store.start()
    for copy in copies[1:]:
        copy.wait()

    @tiles(rows, 256)
    def _(block, i):
        scale = lane_tiled(degree_inv[block, :], width)
        summed = (dot(mix[:, block], images[...], 0, 0) + partial[block, :]) * scale
        aggregated = jnp.tanh(summed)
        opened = gate[block, :]
        row_scale = opened * (1.0 - aggregated * aggregated) * scale
        gate_scale = (
            (aggregated - states[block, :].astype(F32)) * opened * (1.0 - opened)
        )
        alpha[block, :] = row_scale
        beta[block, :] = gate_scale
        upstream = cotangent[block, :].astype(F32)
        row_value = (upstream * row_scale).astype(BF)
        row_grad[block, :] = row_value
        value = (
            upstream * (1.0 - opened)
            + dot(row_value, self_weight[...], 1, 1)
            + dot((upstream * gate_scale).astype(BF), gate_weight[...], 1, 1)
        )
        dense[block, :] = value.astype(dense.dtype)

    store.wait()


def upstream_of(block, i, cotangent, handed, handed_slots, export_row):
    total = cotangent[block, :].astype(F32)
    size = total.shape[0]
    slots = export_row.shape[1]
    row = lax.broadcasted_iota(jnp.int32, (size, slots), 0) + i * size
    hot = ones_where(export_row[...] == row)
    return total + handed[block, :].astype(F32) + dot(hot, handed_slots[...])


def dense_kernel(last, *refs):
    refs = list(refs)
    cotangent, alpha, beta, gate, self_weight, gate_weight = refs[:6]
    refs = refs[6:]
    handed, handed_slots, export_row = refs[:3]
    refs = refs[3:]
    if last:
        row_grad, dense, gate_row, bias = refs
        bias[...] = jnp.zeros_like(bias)
    else:
        row_grad, dense = refs
    rows = cotangent.shape[0]
    size = 256

    @tiles(rows, size)
    def _(block, i):
        upstream = upstream_of(block, i, cotangent, handed, handed_slots, export_row)
        row_value = (upstream * alpha[block, :]).astype(BF)
        gate_value = upstream * beta[block, :]
        gate_small = gate_value.astype(BF)
        row_grad[block, :] = row_value
        value = (
            upstream * (1.0 - gate[block, :])
            + dot(row_value, self_weight[...], 1, 1)
            + dot(gate_small, gate_weight[...], 1, 1)
        )
        dense[block, :] = value.astype(dense.dtype)
        if last:
            gate_row[block, :] = gate_small
            bias[...] += jnp.sum(gate_value, axis=0, keepdims=True)


def slot_kernel(slots, row_grad, mix, basis, slot_grad, mixed):
    width = row_grad.shape[1]
    blocks = basis.shape[1] // width
    part = min(256, slots)

    @tiles(slots, part)
    def _(block, i):
        total = jnp.zeros((part, width), F32)
        for b in range(blocks):
            at = pl.ds(pl.multiple_of(b * slots + i * part, part), part)
            value = dot(mix[at, :], row_grad[...]).astype(BF)
            mixed[at, :] = value
            total += dot(value, basis[:, b * width : (b + 1) * width], 1, 1)
        slot_grad[block, :] = total.astype(BF)


def placer(parts, order):
    me = lax.axis_index("ent")
    even = lax.rem(me, 2) == 0

    def place(i, kept, sent, at, first, second):
        spot = 0
        for k, distance in enumerate(order[1:]):
            mine = lax.rem(lax.div(me, distance), 2)
            bit = 1 - mine if (i // distance) % 2 else mine
            spot = spot + bit * (1 << (len(order) - 2 - k))
        size = first.shape[0]
        kept[spot, at : at + size, :] = jnp.where(even, first, second).astype(BF)
        sent[spot, at : at + size, :] = jnp.where(even, second, first).astype(BF)

    return place


def basis_term(b, slots, received, mixed, coef_t, rel_sum, rel_emb, scaled):
    width = mixed.shape[1]
    scale = lane_tiled(spread_column(coef_t[b : b + 1, :]), width)
    scaled[...] = (scale * rel_sum[...]).astype(BF)
    return dot(received[...], mixed, 0, 0) + dot(rel_emb[...], scaled[...], 0, 0)


def first_weight_kernel(
    slots,
    parts,
    order,
    row_grad,
    gate_row,
    states,
    received,
    mix,
    counts,
    coef_t,
    rel_emb,
    kept,
    sent,
    rel_sum,
    scaled,
    total,
):
    width = states.shape[1]
    cut = width // parts
    place = placer(parts, order)
    rel_sum[...] = dot(counts[...], row_grad[...])

    def put(value, at):
        total[...] = value
        for i in range(0, parts, 2):
            place(
                i,
                kept,
                sent,
                at,
                total[i * cut : (i + 1) * cut, :],
                total[(i + 1) * cut : (i + 2) * cut, :],
            )

    put(dot(states[...], row_grad[...], 0, 0), 0)
    put(dot(states[...], gate_row[...], 0, 0), cut)
    mixed = dot(mix[:slots, :], row_grad[...]).astype(BF)
    put(basis_term(0, slots, received, mixed, coef_t, rel_sum, rel_emb, scaled), 2 * cut)


def second_weight_kernel(
    slots,
    parts,
    order,
    tile_count,
    row_grad,
    received,
    mixed,
    coef_t,
    rel_emb,
    basis,
    bias,
    images,
    rel_sum,
    src_row,
    dst_row,
    rel_row,
    kept,
    sent,
    scaled,
    total,
    edge_grad,
):
    rows, width = row_grad.shape
    blocks, relations = coef_t.shape
    edges = src_row.shape[1]
    cut = width // parts
    rel_cut = relations // parts
    rel_room = rounded_up(rel_cut, 16)
    place = placer(parts, order)
    rel_grad = jnp.zeros((relations, width), F32)
    corner = []
    for b in range(blocks):
        columns = slice(b * width, (b + 1) * width)
        corner.append(
            jnp.sum(
                rel_sum[...] * dot(rel_emb[...], basis[:, columns]),
                axis=1,
                keepdims=True,
            )
        )
        term = basis_term(
            b,
            slots,
            received,
            mixed[b * slots : (b + 1) * slots, :],
            coef_t,
            rel_sum,
            rel_emb,
            scaled,
        ) if b else None
        if not b:
            scale = lane_tiled(spread_column(coef_t[:1, :]), width)
            scaled[...] = (scale * rel_sum[...]).astype(BF)
        rel_grad += dot(scaled[...], basis[:, columns], 1, 1)
        if b:
            total[...] = term
            for i in range(0, parts, 2):
                place(
                    i,
                    kept,
                    sent,
                    (b - 1) * cut,
                    total[i * cut : (i + 1) * cut, :],
                    total[(i + 1) * cut : (i + 2) * cut, :],
                )

    size = 256
    live_edges = tile_count[0, 0] * TILE

    def edge_step(i, sums):
        block = pl.ds(pl.multiple_of(i * size, size), size)
        column = lane_tiled(spread_column(dst_row[:, block]), rows)
        edge = lax.broadcasted_iota(jnp.int32, (size, rows), 0) + i * size
        row = lax.broadcasted_iota(jnp.int32, (size, rows), 1)
        hot = ones_where((column == row) & (edge < live_edges))
        edge_grad[...] = dot(hot, row_grad[...]).astype(BF)
        slot_column = lane_tiled(spread_column(src_row[:, block]), slots)
        own = slot_column == lax.broadcasted_iota(jnp.int32, (size, slots), 1)
        rel_hot = ones_where(
            rel_row[:, block] == lax.broadcasted_iota(jnp.int32, (relations, size), 0)
        )
        lane = lax.broadcasted_iota(jnp.int32, (size, LANES), 1)
        inner = jnp.zeros((size, LANES), F32)
        for b in range(blocks):
            product = dot(edge_grad[...], images[b * slots : (b + 1) * slots, :], 1, 1)
            value = jnp.sum(
                jnp.where(own, product, jnp.float32(0)), axis=1, keepdims=True
            )
            inner = jnp.where(lane == b, value, inner)
        high = inner.astype(BF)
        low = (inner - high.astype(F32)).astype(BF)
        return sums + dot(rel_hot, high) + dot(rel_hot, low)

    gathered = lax.fori_loop(
        0, edges // size, edge_step, jnp.zeros((relations, LANES), F32)
    )
    lane = lax.broadcasted_iota(jnp.int32, (relations, LANES), 1)
    for b in range(blocks):
        gathered = gathered + jnp.where(lane == b, corner[b], jnp.float32(0))
    turned = jnp.transpose(gathered)[:8]
    if relations < width:
        turned = jnp.concatenate(
            [turned, jnp.zeros((8, width - relations), F32)], axis=1
        )
    bias8 = jnp.broadcast_to(bias[...], (8, width))
    at = (blocks - 1) * cut
    rest = kept.shape[1] - at - rel_room

    def last_rows(p):
        lines = [rel_grad[p * rel_cut : (p + 1) * rel_cut]]
        if rel_room > rel_cut:
            lines.append(jnp.zeros((rel_room - rel_cut, width), F32))
        lines.append(turned if p == 0 else pltpu.roll(turned, width - p * rel_cut, 1))
        lines.append(bias8 if p == 0 else pltpu.roll(bias8, width - p * cut, 1))
        if rest > 16:
            lines.append(jnp.zeros((rest - 16, width), F32))
        return jnp.concatenate(lines, axis=0)

    for i in range(0, parts, 2):
        place(i, kept, sent, at, last_rows(i), last_rows(i + 1))


def fold_kernel(kept, taken, next_kept, next_sent):
    left = next_kept.shape[0]
    for spot in range(left):
        next_kept[spot] = (kept[spot].astype(F32) + taken[spot].astype(F32)).astype(BF)
        other = left + spot
        next_sent[spot] = (kept[other].astype(F32) + taken[other].astype(F32)).astype(BF)


def join_kernel(kept_a, taken_a, kept_b, taken_b, joined):
    parts = [
        kept_a[0].astype(F32) + taken_a[0].astype(F32),
        kept_b[0].astype(F32) + taken_b[0].astype(F32),
    ]
    whole = jnp.concatenate(parts, axis=0).astype(BF)
    size = joined.shape[1]
    for k in range(joined.shape[0]):
        joined[k] = whole[k * size : (k + 1) * size]


def quarter_kernel(taken, total):
    value = taken[0].astype(F32)
    for k in range(1, taken.shape[0]):
        value += taken[k].astype(F32)
    total[...] = value.astype(BF)


def final_kernel(final, basis, self_part, gate_part, rel, coef_t, bias):
    cut, width = self_part.shape
    blocks, rel_cut = coef_t.shape
    value = final[...].astype(F32)
    self_part[...] = value[:cut]
    gate_part[...] = value[cut : 2 * cut]
    for b in range(blocks):
        basis[:, b * width : (b + 1) * width] = value[(b + 2) * cut : (b + 3) * cut]
    at = (blocks + 2) * cut
    rel[...] = value[at : at + rel_cut]
    at += rounded_up(rel_cut, 16)
    coef_t[...] = value[at : at + blocks, :rel_cut]
    bias[...] = value[at + 8 : at + 9, :cut]


def output_kernel(dense, returned, export_row, total):
    rows = dense.shape[0]
    slots = export_row.shape[1]
    size = 256

    @tiles(rows, size)
    def _(block, i):
        row = lax.broadcasted_iota(jnp.int32, (size, slots), 0) + i * size
        hot = ones_where(export_row[...] == row)
        total[block, :] = dense[block, :] + dot(hot, returned[...])


def from_next(block, axis):
    count = lax.axis_size(axis)
    return lax.ppermute(block, axis, [(i, i - 1) for i in range(1, count)])


def per_device(
    states,
    cotangent,
    export_rows,
    edge_src,
    edge_dst,
    edge_rel,
    tile_count,
    basis,
    coef,
    rel_emb,
    self_weight,
    gate_weight,
    gate_bias,
):
    ent_count = lax.axis_size("ent")
    section_count = lax.axis_size("tm")
    own = states[0]
    cot = cotangent[0]
    rows, width = own.shape
    blocks = basis.shape[1] // width
    relations = rel_emb.shape[0]
    edges = edge_src.shape[1]
    slots = export_rows.shape[1]
    per_owner = slots // ent_count

    def exchange(block):
        return lax.all_to_all(
            block.reshape(ent_count, per_owner, width), "ent", 0, 0, tiled=True
        ).reshape(slots, width)

    dma = pltpu.SemaphoreType.DMA
    sent = call(
        export_kernel,
        ((slots, width), BF, ANY),
        [(own, ANY), (export_rows, ANY)],
        scratch=(
            VM((rows, width), BF),
            VM((1, slots), jnp.int32),
            VM((slots, width), BF),
            dma((3,)),
        ),
        flops=2 * slots * rows * width,
        limit=FULL,
    )
    received = exchange(sent)
    export_next = from_next(export_rows, "tm")
    coef_t = coef.T
    bias_row = gate_bias[None]
    sources = [
        edge_dst,
        edge_rel,
        edge_src,
        coef_t,
        rel_emb,
        basis,
        own,
        self_weight,
        gate_weight,
        bias_row,
    ]
    made = [
        ((blocks * slots, rows), BF),
        ((relations, rows), BF),
        ((rows, LANES), F32),
        ((rows, width), F32),
        ((rows, width), F32),
    ]
    mix, counts, degree_inv, partial, gate = call(
        functools.partial(setup_kernel, slots),
        [out + (ANY,) for out in made],
        [(tile_count, pltpu.SMEM)] + [(array, ANY) for array in sources],
        scratch=[VM(array.shape, array.dtype) for array in sources]
        + [VM(dims, kind) for dims, kind in made]
        + [
            VM((edges, rows), BF),
            VM((blocks, edges), F32),
            VM((relations, width), BF),
            dma((len(sources),)),
            dma((len(made),)),
        ],
        flops=2 * blocks * slots * rows * edges,
        limit=FULL,
    )
    outs = call(
        functools.partial(forward_kernel, slots),
        [
            (basis.shape, BF, VM),
            (mix.shape, BF, VM),
            ((rows, width), F32, VM),
            ((width, width), BF, VM),
            ((width, width), BF, VM),
            ((rows, width), BF, VM),
            ((rows, width), F32, VM),
            ((rows, width), F32, VM),
            ((rows, width), BF, VM),
            ((rows, width), BF, VM),
            ((blocks * slots, width), BF, ANY),
        ],
        [(received, VM)]
        + [
            (array, ANY)
            for array in (
                basis,
                mix,
                degree_inv,
                partial,
                gate,
                own,
                cot,
                self_weight,
                gate_weight,
            )
        ],
        scratch=[
            VM((rows, width), F32),
            VM((rows, LANES), F32),
            VM((rows, width), BF),
            VM((blocks * slots, width), BF),
            dma((10,)),
        ],
        flops=4 * blocks * slots * rows * width,
        limit=FULL - (16 << 20),
    )
    basis_near, mix_near, gate_near, self_near, gate_weight_near, cot_near = outs[:6]
    alpha, beta, row_grad, dense, images = outs[6:]

    def slot_step(row_grad):
        return call(
            functools.partial(slot_kernel, slots),
            [((slots, width), BF, VM), ((blocks * slots, width), BF, VM)],
            [(row_grad, VM), (mix_near, VM), (basis_near, VM)],
            flops=4 * blocks * slots * rows * width,
        )

    for step in range(1, section_count):
        last = step + 1 == section_count
        slot_grad, _ = slot_step(row_grad)
        ahead = from_next(dense, "tm")
        returned = from_next(exchange(slot_grad), "tm")
        args = [cot_near, alpha, beta, gate_near, self_near, gate_weight_near]
        args += [ahead, returned, export_next]
        outs = [((rows, width), BF, VM), ((rows, width), F32 if last else BF, VM)]
        if last:
            outs += [((rows, width), BF, VM), ((1, width), F32, VM)]
        outs = call(
            functools.partial(dense_kernel, last),
            outs,
            [(array, VM) for array in args],
            flops=4 * rows * width * width,
        )
        row_grad, dense = outs[:2]
    gate_row, bias = outs[2:]

    cut, rel_cut = width // ent_count, relations // ent_count
    first_depth = 3 * cut
    rest = (blocks - 1) * cut + rounded_up(rel_cut, 16) + 16
    depth = rounded_up(first_depth + rest, 16 * section_count)
    distances = []
    while 1 << len(distances) < ent_count:
        distances.append(1 << len(distances))
    orders = (distances, distances[:1] + distances[:0:-1])
    half = ent_count // 2
    kept_a, sent_a, rel_sum = call(
        functools.partial(first_weight_kernel, slots, ent_count, orders[0]),
        [
            ((half, first_depth, width), BF, VM),
            ((half, first_depth, width), BF, VM),
            ((relations, width), F32, VM),
        ],
        [
            (array, VM)
            for array in (
                row_grad,
                gate_row,
                own,
                received,
                mix_near,
                counts,
                coef_t,
                rel_emb,
            )
        ],
        scratch=[VM((relations, width), BF), VM((width, width), F32)],
        flops=4 * rows * width * width,
    )
    slot_grad, mixed = slot_step(row_grad)
    kept_b, sent_b = call(
        functools.partial(second_weight_kernel, slots, ent_count, orders[1]),
        [((half, depth - first_depth, width), BF, VM)] * 2,
        [(tile_count, pltpu.SMEM)]
        + [
            (array, VM)
            for array in (
                row_grad,
                received,
                mixed,
                coef_t,
                rel_emb,
                basis_near,
                bias,
                images,
                rel_sum,
                edge_src,
                edge_dst,
                edge_rel,
            )
        ],
        scratch=[
            VM((relations, width), BF),
            VM((width, width), F32),
            VM((256, width), BF),
        ],
        flops=8 * blocks * slots * rows * width,
    )
    folds = [(kept_a, sent_a), (kept_b, sent_b)]
    taken = [None, None]
    for k in range(len(distances)):
        for which in range(2):
            kept, moved = folds[which]
            distance = orders[which][k]
            route = [(i, i ^ distance) for i in range(ent_count)]
            taken[which] = lax.ppermute(moved, "ent", route)
        if k + 1 < len(distances):
            for which in range(2):
                kept = folds[which][0]
                dims = (kept.shape[0] // 2,) + kept.shape[1:]
                folds[which] = call(
                    fold_kernel,
                    [(dims, BF, VM)] * 2,
                    [(kept, VM), (taken[which], VM)],
                    flops=1 << 20,
                )
    joined = call(
        join_kernel,
        ((section_count, depth // section_count, width), BF, VM),
        [(folds[0][0], VM), (taken[0], VM), (folds[1][0], VM), (taken[1], VM)],
        flops=1 << 20,
    )
    returned = exchange(slot_grad)
    state_grad = call(
        output_kernel,
        ((rows, width), F32, VM),
        [(dense, VM), (returned, VM), (export_rows, VM)],
        flops=2 * rows * slots * width,
    )
    quarter = call(
        quarter_kernel,
        ((depth // section_count, width), BF, VM),
        [(lax.all_to_all(joined, "tm", 0, 0, tiled=True), VM)],
        flops=1 << 20,
    )
    final = lax.all_gather(quarter, "tm", axis=0, tiled=True)
    grad_basis, grad_self, grad_gate, grad_rel, grad_coef, grad_bias = call(
        final_kernel,
        [
            ((cut, blocks * width), F32, VM),
            ((cut, width), F32, VM),
            ((cut, width), F32, VM),
            ((rel_cut, width), F32, VM),
            ((blocks, rel_cut), F32, VM),
            ((1, cut), F32, VM),
        ],
        [(final, VM)],
        flops=1 << 20,
    )
    return (
        state_grad[None],
        grad_basis,
        grad_self,
        grad_gate,
        grad_bias[0],
        grad_coef.T,
        grad_rel,
    )


def solution(mesh):
    placed = (P("tm", "ent", None),) * 2 + (P("tm", "ent"),) * 5 + (P(),) * 6
    return jax.shard_map(
        per_device,
        mesh=mesh,
        in_specs=placed,
        out_specs=(
            P("tm", "ent", None),
            P("ent", None),
            P("ent", None),
            P("ent", None),
            P("ent"),
            P("ent", None),
            P("ent", None),
        ),
        check_vma=False,
    )
```

time: 259 us -> 217 us (0.84)
  local copies, waits for them, and re-layouts: 38.5 us -> 5.32 us
  waiting for transfers between devices: 91.8 us -> 75.8 us
  Pallas kernels: 48.1 us -> 58.7 us
  other arithmetic: 6.08 us -> 0 us
  starting transfers between devices: 23.6 us -> 27.4 us
    unnamed x97 -> x34, local copies, waits for them, and re-layouts: 34.2 us -> 5.32 us
    ppermute x3 -> x6, waiting for transfers between devices: 35.3 us -> 21 us  [per_device(): taken[which] = lax.ppermute(moved, 'ent', route)]
    pallas_call x13 -> x20, Pallas kernels: 48.1 us -> 58.7 us  [call(): pl.pallas_call(kernel, out_shape=out_shape[0] if single else out_shape, i...]
    convert_element_type x4 -> x0, other arithmetic: 6.01 us -> none  [the longest x2 4.01 us: halve_over(): values = values.astype(BF)]
    ppermute x3 -> x6, starting transfers between devices: 1.86 us -> 5.75 us  [per_device(): taken[which] = lax.ppermute(moved, 'ent', route)]
    ppermute x7, waiting for transfers between devices: 47.3 us -> 44.2 us  [from_next(): return lax.ppermute(block, axis, [(i, i - 1) for i in range(1, count)])]
  transfers between devices with their start and end apart: 13 -> 16, of which waited for: 7 -> 7; matrix products, arithmetic and copies ran while one was open for 1% -> 0% of each run, Pallas kernels for 7% -> 11%
where the time goes in v2:
time: 217 us; the launch traced here: 216 us
  waiting for transfers between devices  75.8 us (35%)
  Pallas kernels  58.7 us (27%)
  blocking collectives  46.9 us (22%)
  starting transfers between devices  27.4 us (13%)
  local copies, waits for them, and re-layouts  5.32 us (2%)
    pallas_call x20, Pallas kernels, call(): pl.pallas_call(kernel, out_shape=out_shape[0] if single else out_shape, i...  58.7 us
    ppermute x7, waiting for transfers between devices, from_next(): return lax.ppermute(block, axis, [(i, i - 1) for i in range(1, count)])  44.2 us
    all_to_all x3, blocking collectives, exchange(): lax.all_to_all(block.reshape(ent_count, per_owner, width), 'ent', 0, 0, t...  31.5 us
    ppermute x6, waiting for transfers between devices, per_device(): taken[which] = lax.ppermute(moved, 'ent', route)  21 us
    all_gather x1, blocking collectives, per_device(): final = lax.all_gather(quarter, 'tm', axis=0, tiled=True)  15.4 us
    all_to_all x1, waiting for transfers between devices, per_device(): lax.all_to_all(joined, 'tm', 0, 0, tiled=True)  10.6 us
    ppermute x7, starting transfers between devices, from_next(): return lax.ppermute(block, axis, [(i, i - 1) for i in range(1, count)])  9.19 us
    all_to_all x2, starting transfers between devices, exchange(): lax.all_to_all(block.reshape(ent_count, per_owner, width), 'ent', 0, 0, t...  8.62 us
  transfers between devices with their start and end apart: 16, of which 7 were waited for; matrix products, arithmetic and copies ran while one was open for 0% of the time, Pallas kernels for 11%

profile of v2, /device:TPU:0, one launch (start us, length us, event | category | flops | bytes accessed | tf_op | source)
XLA Modules:
  0.0 215.8 jit_solution(278603573922907880)
XLA Ops:
  0.6 2.5 %shard_map.180 = bf16[256,512]{1,0:T(8,128)(2,1)} custom-call(bf16[1024,512]{1,0:T(8,128)(2,1)} %bitcast.17, s32[1,256]{1,0:T(1,128)} %export_row.1), custom_call_target="tpu_custom_call" | custom-call | flops 268435456 | bytes 4194304 | tf_op jit(solution)/shard_map/pallas_call | solution.py:48
  3.1 5.2 %all-to-all-start = ((bf16[8,32,512]{2,1,0:T(8,128)(2,1)}), bf16[8,32,512]{2,1,0:T(8,128)(2,1)S(1)}, u32[]{:S(2)}, u32[]{:S(2)}) async-start(bf16[8,32,512]{2,1,0:T(8,128)(2,1)} %bitcast.33), calls=%async_computation | async-start | bytes 524288 | tf_op jit(solution)/shard_map/all_to_all | solution.py:571
  9.0 9.9 %shard_map.181 = (bf16[1024,1024]{1,0:T(8,128)(2,1)}, bf16[256,1024]{1,0:T(8,128)(2,1)}, f32[1024,128]{1,0:T(8,128)}, f32[1024,512]{1,0:T(8,128)}, f32[1024,512]{1,0:T(8,128)}) custom-call(s32[1,1]{1,0:T(1,128)S(6)} %copy.20.refs_0_.tile_count, s32[1,1024]{1,0:T(1,128)} %dst_row.1, s32[1,1024]{1,0:T(1,128)} %rel_row.1, s32[1,1024]{1,0:T(1,128)} %src_row.1, ...), custom_call_target="tpu_custom_call" | custom-call | flops 2147483648 | bytes 4194304 | tf_op jit(solution)/shard_map/pallas_call | solution.py:48
  21.0 11.7 %shard_map.182 = (bf16[512,2048]{1,0:T(8,128)(2,1)}, bf16[1024,1024]{1,0:T(8,128)(2,1)}, f32[1024,512]{1,0:T(8,128)}, bf16[512,512]{1,0:T(8,128)(2,1)S(1)}, bf16...) custom-call(bf16[256,512]{1,0:T(8,128)(2,1)S(1)} %bitcast.21, ...), custom_call_target="tpu_custom_call" | custom-call | flops 2147483648 | bytes 4194304 | tf_op jit(solution)/shard_map/pallas_call | solution.py:48
  37.2 2.9 %shard_map.183 = (bf16[256,512]{1,0:T(8,128)(2,1)S(1)}, bf16[1024,512]{1,0:T(8,128)(2,1)}) custom-call(bf16[1024,512]{1,0:T(8,128)(2,1)S(1)} %get-tuple-element.66.row_grad, bf16[1024,1024]{1,0:T(8,128)(2,1)S(1)} %copy-done.4, bf16[512,2048]{1,0:T(8,128)(2,1)S(1)} %copy-done.12), custom_call_target="tpu_custom_call" | custom-call | flops 2147483648 | bytes 4194304 | tf_op jit(solution)/shard_map/pallas_call | solution.py:48
  40.1 10.9 %all_to_all.30 = bf16[8,32,512]{2,1,0:T(8,128)(2,1)S(1)} all-to-all(bf16[8,32,512]{2,1,0:T(8,128)(2,1)S(1)} %bitcast.25), channel_id=1, replica_groups=mesh['tm'=4,'ent'=8] {'ent'}, dimensions={0} | all-to-all | bytes 524288 | tf_op jit(solution)/shard_map/all_to_all | solution.py:571
  53.6 12.3 %collective-permute-done.2.refs_8_ = s32[1,256]{1,0:T(1,128)S(1)} collective-permute-done((s32[1,256]{1,0:T(1,128)S(1)}, s32[1,256]{1,0:T(1,128)S(1)}, u32[]{:S(2)}, u32[]{:S(2)}) %collective-permute-start.2) | collective-permute-done | bytes 1056 | tf_op jit(solution)/shard_map/ppermute | solution.py:541
  65.9 2.4 %shard_map.184 = (bf16[1024,512]{1,0:T(8,128)(2,1)S(1)}, bf16[1024,512]{1,0:T(8,128)(2,1)S(1)}) custom-call(bf16[1024,512]{1,0:T(8,128)(2,1)S(1)} %get-tuple-element.59.refs_0_, f32[1024,512]{1,0:T(8,128)S(1)} %copy-done.1, f32[1024,512]{1,0:T(8,128)S(1)} %copy-done.2, f32[1024,512]{1,0:T(8,128)S(1)} %copy-done, ...), custom_call_target="tpu_custom_call" | custom-call | flops 1073741824 | bytes 4194304 | tf_op jit(solution)/shard_map/pallas_call | solution.py:48
  69.6 2.8 %shard_map.185 = (bf16[256,512]{1,0:T(8,128)(2,1)S(1)}, bf16[1024,512]{1,0:T(8,128)(2,1)}) custom-call(bf16[1024,512]{1,0:T(8,128)(2,1)S(1)} %get-tuple-element.71.row_grad, bf16[1024,1024]{1,0:T(8,128)(2,1)S(1)} %copy-done.4, bf16[512,2048]{1,0:T(8,128)(2,1)S(1)} %copy-done.12), custom_call_target="tpu_custom_call" | custom-call | flops 2147483648 | bytes 4194304 | tf_op jit(solution)/shard_map/pallas_call | solution.py:48
  72.4 10.5 %all_to_all.31 = bf16[8,32,512]{2,1,0:T(8,128)(2,1)S(1)} all-to-all(bf16[8,32,512]{2,1,0:T(8,128)(2,1)S(1)} %bitcast.26), channel_id=1, replica_groups=mesh['tm'=4,'ent'=8] {'ent'}, dimensions={0} | all-to-all | bytes 524288 | tf_op jit(solution)/shard_map/all_to_all | solution.py:571
  84.2 16.3 %collective-permute-done.4.refs_7_ = bf16[256,512]{1,0:T(8,128)(2,1)S(1)} collective-permute-done((bf16[256,512]{1,0:T(8,128)(2,1)S(1)}, bf16[256,512]{1,0:T(8,128)(2,1)S(1)}, u32[]{:S(2)}, u32[]{:S(2)}) %collective-permute-start.4) | collective-permute-done | bytes 262176 | tf_op jit(solution)/shard_map/ppermute | solution.py:541
  100.5 2.4 %shard_map.186 = (bf16[1024,512]{1,0:T(8,128)(2,1)S(1)}, bf16[1024,512]{1,0:T(8,128)(2,1)S(1)}) custom-call(bf16[1024,512]{1,0:T(8,128)(2,1)S(1)} %get-tuple-element.59.refs_0_, f32[1024,512]{1,0:T(8,128)S(1)} %copy-done.1, f32[1024,512]{1,0:T(8,128)S(1)} %copy-done.2, f32[1024,512]{1,0:T(8,128)S(1)} %copy-done, ...), custom_call_target="tpu_custom_call" | custom-call | flops 1073741824 | bytes 4194304 | tf_op jit(solution)/shard_map/pallas_call | solution.py:48
  104.3 2.8 %shard_map.187 = (bf16[256,512]{1,0:T(8,128)(2,1)S(1)}, bf16[1024,512]{1,0:T(8,128)(2,1)}) custom-call(bf16[1024,512]{1,0:T(8,128)(2,1)S(1)} %get-tuple-element.74.row_grad, bf16[1024,1024]{1,0:T(8,128)(2,1)S(1)} %copy-done.4, bf16[512,2048]{1,0:T(8,128)(2,1)S(1)} %copy-done.12), custom_call_target="tpu_custom_call" | custom-call | flops 2147483648 | bytes 4194304 | tf_op jit(solution)/shard_map/pallas_call | solution.py:48
  107.2 10.1 %all_to_all.32 = bf16[8,32,512]{2,1,0:T(8,128)(2,1)S(1)} all-to-all(bf16[8,32,512]{2,1,0:T(8,128)(2,1)S(1)} %bitcast.27), channel_id=1, replica_groups=mesh['tm'=4,'ent'=8] {'ent'}, dimensions={0} | all-to-all | bytes 524288 | tf_op jit(solution)/shard_map/all_to_all | solution.py:571
  118.5 15.7 %collective-permute-done.6.refs_7_ = bf16[256,512]{1,0:T(8,128)(2,1)S(1)} collective-permute-done((bf16[256,512]{1,0:T(8,128)(2,1)S(1)}, bf16[256,512]{1,0:T(8,128)(2,1)S(1)}, u32[]{:S(2)}, u32[]{:S(2)}) %collective-permute-start.6) | collective-permute-done | bytes 262176 | tf_op jit(solution)/shard_map/ppermute | solution.py:541
  134.2 2.7 %shard_map.188 = (bf16[1024,512]{1,0:T(8,128)(2,1)S(1)}, f32[1024,512]{1,0:T(8,128)S(1)}, bf16[1024,512]{1,0:T(8,128)(2,1)S(1)}, f32[1,512]{1,0:T(1,128)S(1)}) custom-call(bf16[1024,512]{1,0:T(8,128)(2,1)S(1)} %get-tuple-element.59.refs_0_, f32[1024,512]{1,0:T(8,128)S(1)} %copy-done.1, f32[1024,512]{1,0:T(8,128)S(1)} %copy-done.2, f32[1024,512]{1,0:T(8,128)S(1)} %copy-done, ...), custom_call_target="tpu_custom_call" | custom-call | flops 1073741824 | bytes 4194304 | tf_op jit(solution)/shard_map/pallas_call | solution.py:48
  136.9 2.7 %shard_map.189 = (bf16[256,512]{1,0:T(8,128)(2,1)}, bf16[1024,512]{1,0:T(8,128)(2,1)S(1)}) custom-call(bf16[1024,512]{1,0:T(8,128)(2,1)S(1)} %get-tuple-element.77.row_grad, bf16[1024,1024]{1,0:T(8,128)(2,1)S(1)} %copy-done.4, bf16[512,2048]{1,0:T(8,128)(2,1)S(1)} %copy-done.12), custom_call_target="tpu_custom_call" | custom-call | flops 2147483648 | bytes 4194304 | tf_op jit(solution)/shard_map/pallas_call | solution.py:48
  141.9 6.8 %shard_map.194 = (bf16[4,256,512]{2,1,0:T(8,128)(2,1)S(1)}, bf16[4,256,512]{2,1,0:T(8,128)(2,1)S(1)}) custom-call(s32[1,1]{1,0:T(1,128)S(6)} %copy.20.refs_0_.tile_count, bf16[1024,512]{1,0:T(8,128)(2,1)S(1)} %get-tuple-element.77.row_grad, bf16[256,512]{1,0:T(8,128)(2,1)S(1)} %bitcast.23, bf16[1024,512]{1,0:T(8,128)(2,1)S(1)} %get-tuple-element.87.mixed, ...), custom_call_target="tpu_custom_call" | custom-call | flops 4294967296 | bytes 4194304 | tf_op jit(solution)/shard_map/pallas_call | solution.py:48
  154.9 10.8 %collective-permute-done.11.taken = bf16[2,256,512]{2,1,0:T(8,128)(2,1)S(1)} collective-permute-done((bf16[2,256,512]{2,1,0:T(8,128)(2,1)S(1)}, bf16[2,256,512]{2,1,0:T(8,128)(2,1)S(1)}, u32[]{:S(2)}, u32[]{:S(2)}) %collective-permute-start.11) | collective-permute-done | bytes 524320 | tf_op jit(solution)/shard_map/ppermute | solution.py:766
  167.3 3.4 %all-to-all-start.4 = ((bf16[8,32,512]{2,1,0:T(8,128)(2,1)}), bf16[8,32,512]{2,1,0:T(8,128)(2,1)S(1)}, u32[]{:S(2)}, u32[]{:S(2)}) async-start(bf16[8,32,512]{2,1,0:T(8,128)(2,1)} %bitcast.12), calls=%async_computation.4 | async-start | bytes 524288 | tf_op jit(solution)/shard_map/all_to_all | solution.py:571
  172.8 8.0 %collective-permute-done.9.taken_a = bf16[1,192,512]{2,1,0:T(8,128)(2,1)S(1)} collective-permute-done((bf16[1,192,512]{2,1,0:T(8,128)(2,1)S(1)}, bf16[1,192,512]{2,1,0:T(8,128)(2,1)S(1)}, u32[]{:S(2)}, u32[]{:S(2)}) %collective-permute-start.9) | collective-permute-done | bytes 196640 | tf_op jit(solution)/shard_map/ppermute | solution.py:766
  182.7 3.9 %all-to-all-start.5 = ((bf16[4,112,512]{2,1,0:T(8,128)(2,1)}), bf16[4,112,512]{2,1,0:T(8,128)(2,1)S(1)}, u32[]{:S(2)}, u32[]{:S(2)}) async-start(bf16[4,112,512]{2,1,0:T(8,128)(2,1)} %shard_map.197), calls=%async_computation.5 | async-start | bytes 917504 | tf_op jit(solution)/shard_map/all_to_all | solution.py:793
  188.8 10.6 %all-to-all-done.5.taken = bf16[4,112,512]{2,1,0:T(8,128)(2,1)S(1)} async-done(((bf16[4,112,512]{2,1,0:T(8,128)(2,1)}), bf16[4,112,512]{2,1,0:T(8,128)(2,1)S(1)}, u32[]{:S(2)}, u32[]{:S(2)}) %all-to-all-start.5) | async-done | bytes 458784 | tf_op jit(solution)/shard_map/all_to_all | solution.py:793
  199.4 15.4 %all_gather.3.final = bf16[448,512]{1,0:T(8,128)(2,1)S(1)} all-gather(bf16[112,512]{1,0:T(8,128)(2,1)S(1)} %shard_map.198), channel_id=1, replica_groups=mesh['tm'=4,'ent'=8] {'tm'}, dimensions={0}, use_global_device_ids=true | all-gather | bytes 573440 | tf_op jit(solution)/shard_map/all_gather | solution.py:796
  (66 shorter events, 31.6 us)
Async XLA Ops:
  3.1 15.8 %all-to-all-start = ((bf16[8,32,512]{2,1,0:T(8,128)(2,1)}), bf16[8,32,512]{2,1,0:T(8,128)(2,1)S(1)}, u32[]{:S(2)}, u32[]{:S(2)}) async-start(bf16[8,32,512]{2,1,0:T(8,128)(2,1)} %bitcast.33), calls=%async_computation | async-start | bytes 524288 | tf_op jit(solution)/shard_map/all_to_all | solution.py:571
  9.0 9.9 %copy-start.5 = (bf16[512,512]{1,0:T(8,128)(2,1)S(1)}, bf16[512,512]{1,0:T(8,128)(2,1)}, u32[]{:S(2)}) copy-start(bf16[512,512]{1,0:T(8,128)(2,1)} %refs_8_.3) | copy-start | bytes 1572868
  32.7 33.2 %collective-permute-start = (bf16[1024,512]{1,0:T(8,128)(2,1)S(1)}, bf16[1024,512]{1,0:T(8,128)(2,1)S(1)}, u32[]{:S(2)}, u32[]{:S(2)}) collective-permute-start(bf16[1024,512]{1,0:T(8,128)(2,1)S(1)} %get-tuple-element.65), channel_id=1, source_target_pairs={{8,0},{16,8},{24,16},{9,1},{17,9},{25,17},{10,2},{18,10},{26,18},{... | collective-permute-start | bytes 3145736 | tf_op jit(solution)/shard_map/ppermute | solution.py:541
  37.2 15.1 %copy-start.10 = (s32[1,256]{1,0:T(1,128)S(1)}, s32[1,256]{1,0:T(1,128)}, u32[]{:S(2)}) copy-start(s32[1,256]{1,0:T(1,128)} %export_row.1) | copy-start | bytes 3076
  37.2 28.7 %copy-start = (f32[1024,512]{1,0:T(8,128)S(1)}, f32[1024,512]{1,0:T(8,128)}, u32[]{:S(2)}) copy-start(f32[1024,512]{1,0:T(8,128)} %get-tuple-element.62.refs_3_) | copy-start | bytes 6291460
  37.2 28.7 %copy-start.1 = (f32[1024,512]{1,0:T(8,128)S(1)}, f32[1024,512]{1,0:T(8,128)}, u32[]{:S(2)}) copy-start(f32[1024,512]{1,0:T(8,128)} %get-tuple-element.60.refs_1_) | copy-start | bytes 6291460
  37.2 28.7 %copy-start.2 = (f32[1024,512]{1,0:T(8,128)S(1)}, f32[1024,512]{1,0:T(8,128)}, u32[]{:S(2)}) copy-start(f32[1024,512]{1,0:T(8,128)} %get-tuple-element.61.refs_2_) | copy-start | bytes 6291460
  51.0 14.9 %collective-permute-start.1 = (bf16[256,512]{1,0:T(8,128)(2,1)S(1)}, bf16[256,512]{1,0:T(8,128)(2,1)S(1)}, u32[]{:S(2)}, u32[]{:S(2)}) collective-permute-start(bf16[256,512]{1,0:T(8,128)(2,1)S(1)} %bitcast.34), channel_id=1, source_target_pairs={{8,0},{16,8},{24,16},{9,1},{17,9},{25,17},{10,2},{18,10},{26,18},{... | collective-permute-start | bytes 786440 | tf_op jit(solution)/shard_map/ppermute | solution.py:541
  52.3 13.6 %collective-permute-start.2 = (s32[1,256]{1,0:T(1,128)S(1)}, s32[1,256]{1,0:T(1,128)S(1)}, u32[]{:S(2)}, u32[]{:S(2)}) collective-permute-start(s32[1,256]{1,0:T(1,128)S(1)} %copy-done.10), channel_id=1, source_target_pairs={{8,0},{16,8},{24,16},{9,1},{17,9},{25,17},{10,2},{18,10},{26,18},{... | collective-permute-start | bytes 3080 | tf_op jit(solution)/shard_map/ppermute | solution.py:541
  68.3 32.2 %collective-permute-start.3 = (bf16[1024,512]{1,0:T(8,128)(2,1)S(1)}, bf16[1024,512]{1,0:T(8,128)(2,1)S(1)}, u32[]{:S(2)}, u32[]{:S(2)}) collective-permute-start(bf16[1024,512]{1,0:T(8,128)(2,1)S(1)} %get-tuple-element.70), channel_id=1, source_target_pairs={{8,0},{16,8},{24,16},{9,1},{17,9},{25,17},{10,2},{18,10},{26,18},{... | collective-permute-start | bytes 3145736 | tf_op jit(solution)/shard_map/ppermute | solution.py:541
  82.9 17.6 %collective-permute-start.4 = (bf16[256,512]{1,0:T(8,128)(2,1)S(1)}, bf16[256,512]{1,0:T(8,128)(2,1)S(1)}, u32[]{:S(2)}, u32[]{:S(2)}) collective-permute-start(bf16[256,512]{1,0:T(8,128)(2,1)S(1)} %bitcast.35), channel_id=1, source_target_pairs={{8,0},{16,8},{24,16},{9,1},{17,9},{25,17},{10,2},{18,10},{26,18},{... | collective-permute-start | bytes 786440 | tf_op jit(solution)/shard_map/ppermute | solution.py:541
  102.9 31.3 %collective-permute-start.5 = (bf16[1024,512]{1,0:T(8,128)(2,1)S(1)}, bf16[1024,512]{1,0:T(8,128)(2,1)S(1)}, u32[]{:S(2)}, u32[]{:S(2)}) collective-permute-start(bf16[1024,512]{1,0:T(8,128)(2,1)S(1)} %get-tuple-element.73), channel_id=1, source_target_pairs={{8,0},{16,8},{24,16},{9,1},{17,9},{25,17},{10,2},{18,10},{26,18},{... | collective-permute-start | bytes 3145736 | tf_op jit(solution)/shard_map/ppermute | solution.py:541
  117.2 16.9 %collective-permute-start.6 = (bf16[256,512]{1,0:T(8,128)(2,1)S(1)}, bf16[256,512]{1,0:T(8,128)(2,1)S(1)}, u32[]{:S(2)}, u32[]{:S(2)}) collective-permute-start(bf16[256,512]{1,0:T(8,128)(2,1)S(1)} %bitcast.36), channel_id=1, source_target_pairs={{8,0},{16,8},{24,16},{9,1},{17,9},{25,17},{10,2},{18,10},{26,18},{... | collective-permute-start | bytes 786440 | tf_op jit(solution)/shard_map/ppermute | solution.py:541
  136.9 2.8 %copy-start.3 = (bf16[1,1024,512]{2,1,0:T(8,128)(2,1)S(1)}, bf16[1,1024,512]{2,1,0:T(8,128)(2,1)}, u32[]{:S(2)}) copy-start(bf16[1,1024,512]{2,1,0:T(8,128)(2,1)} %param.13) | copy-start | bytes 3145732
  136.9 2.8 %copy-start.8 = (bf16[256,1024]{1,0:T(8,128)(2,1)S(1)}, bf16[256,1024]{1,0:T(8,128)(2,1)}, u32[]{:S(2)}) copy-start(bf16[256,1024]{1,0:T(8,128)(2,1)} %get-tuple-element.80.counts) | copy-start | bytes 1572868
  136.9 2.8 %copy-start.9 = (bf16[256,512]{1,0:T(8,128)(2,1)S(1)}, bf16[256,512]{1,0:T(8,128)(2,1)}, u32[]{:S(2)}) copy-start(bf16[256,512]{1,0:T(8,128)(2,1)} %rel_emb.3) | copy-start | bytes 786436
  148.7 2.7 %collective-permute-start.10 = (bf16[4,256,512]{2,1,0:T(8,128)(2,1)S(1)}, bf16[4,256,512]{2,1,0:T(8,128)(2,1)S(1)}, u32[]{:S(2)}, u32[]{:S(2)}) collective-permute-start(bf16[4,256,512]{2,1,0:T(8,128)(2,1)S(1)} %get-tuple-element.92), channel_id=1, source_target_pairs={{0,1},{1,0},{2,3},{3,2},{4,5},{5,4},{6,7},{7,6},{8,9},{9,8},{10,11... | collective-permute-start | bytes 3145736 | tf_op jit(solution)/shard_map/ppermute | solution.py:766
  148.8 3.8 %collective-permute-start.7 = (bf16[4,192,512]{2,1,0:T(8,128)(2,1)S(1)}, bf16[4,192,512]{2,1,0:T(8,128)(2,1)S(1)}, u32[]{:S(2)}, u32[]{:S(2)}) collective-permute-start(bf16[4,192,512]{2,1,0:T(8,128)(2,1)S(1)} %get-tuple-element.82), channel_id=1, source_target_pairs={{0,1},{1,0},{2,3},{3,2},{4,5},{5,4},{6,7},{7,6},{8,9},{9,8},{10,11... | collective-permute-start | bytes 2359304 | tf_op jit(solution)/shard_map/ppermute | solution.py:766
  151.7 14.0 %collective-permute-start.11 = (bf16[2,256,512]{2,1,0:T(8,128)(2,1)S(1)}, bf16[2,256,512]{2,1,0:T(8,128)(2,1)S(1)}, u32[]{:S(2)}, u32[]{:S(2)}) collective-permute-start(bf16[2,256,512]{2,1,0:T(8,128)(2,1)S(1)} %get-tuple-element.94), channel_id=1, source_target_pairs={{0,4},{1,5},{2,6},{3,7},{4,0},{5,1},{6,2},{7,3},{8,12},{9,13},{10,... | collective-permute-start | bytes 1572872 | tf_op jit(solution)/shard_map/ppermute | solution.py:766
  153.4 17.3 %collective-permute-start.8 = (bf16[2,192,512]{2,1,0:T(8,128)(2,1)}, bf16[2,192,512]{2,1,0:T(8,128)(2,1)S(1)}, u32[]{:S(2)}, u32[]{:S(2)}) collective-permute-start(bf16[2,192,512]{2,1,0:T(8,128)(2,1)} %get-tuple-element.84), channel_id=1, source_target_pairs={{0,2},{1,3},{2,0},{3,1},{4,6},{5,7},{6,4},{7,5},{8,10},{9,11},{10,... | collective-permute-start | bytes 1179656 | tf_op jit(solution)/shard_map/ppermute | solution.py:766
  166.5 14.4 %collective-permute-start.12 = (bf16[1,256,512]{2,1,0:T(8,128)(2,1)}, bf16[1,256,512]{2,1,0:T(8,128)(2,1)}, u32[]{:S(2)}, u32[]{:S(2)}) collective-permute-start(bf16[1,256,512]{2,1,0:T(8,128)(2,1)} %get-tuple-element.96), channel_id=1, source_target_pairs={{0,2},{1,3},{2,0},{3,1},{4,6},{5,7},{6,4},{7,5},{8,10},{9,11},{10,... | collective-permute-start | bytes 786440 | tf_op jit(solution)/shard_map/ppermute | solution.py:766
  167.3 15.4 %all-to-all-start.4 = ((bf16[8,32,512]{2,1,0:T(8,128)(2,1)}), bf16[8,32,512]{2,1,0:T(8,128)(2,1)S(1)}, u32[]{:S(2)}, u32[]{:S(2)}) async-start(bf16[8,32,512]{2,1,0:T(8,128)(2,1)} %bitcast.12), calls=%async_computation.4 | async-start | bytes 524288 | tf_op jit(solution)/shard_map/all_to_all | solution.py:571
  170.8 10.0 %collective-permute-start.9 = (bf16[1,192,512]{2,1,0:T(8,128)(2,1)S(1)}, bf16[1,192,512]{2,1,0:T(8,128)(2,1)S(1)}, u32[]{:S(2)}, u32[]{:S(2)}) collective-permute-start(bf16[1,192,512]{2,1,0:T(8,128)(2,1)S(1)} %get-tuple-element.86), channel_id=1, source_target_pairs={{0,4},{1,5},{2,6},{3,7},{4,0},{5,1},{6,2},{7,3},{8,12},{9,13},{10,... | collective-permute-start | bytes 589832 | tf_op jit(solution)/shard_map/ppermute | solution.py:766
  182.7 16.7 %all-to-all-start.5 = ((bf16[4,112,512]{2,1,0:T(8,128)(2,1)}), bf16[4,112,512]{2,1,0:T(8,128)(2,1)S(1)}, u32[]{:S(2)}, u32[]{:S(2)}) async-start(bf16[4,112,512]{2,1,0:T(8,128)(2,1)} %shard_map.197), calls=%async_computation.5 | async-start | bytes 917504 | tf_op jit(solution)/shard_map/all_to_all | solution.py:793
  (9 other events, 16.7 us)

commit v3 on v2

--- a/solution.py
+++ b/solution.py
@@ -38,6 +38,7 @@
 
 ANY = pltpu.HBM
 FULL = 63 << 20
+LIGHT = 1 << 20
 
 
 def call(kernel, outs, args, scratch=(), flops=0, limit=12 << 20):
@@ -105,16 +106,13 @@
 
 def setup_kernel(slots, *refs):
     tile_count = refs[0]
-    sources = refs[1:11]
-    outs = refs[11:16]
-    places = refs[16:26]
-    results = refs[26:31]
-    target, edge_coef, rel_images, in_sems, out_sems = refs[31:]
-    dst_row, rel_row, src_row, coef_t, rel_emb, basis = places[:6]
-    states, self_weight, gate_weight, gate_bias = places[6:]
-    mix, counts, degree_inv, partial, gate = results
-    rows, width = states.shape
-    edges = src_row.shape[1]
+    sources, outs = refs[1:7], refs[7:11]
+    places, results = refs[11:17], refs[17:21]
+    target, edge_coef, in_sems, out_sems = refs[21:]
+    dst_row, rel_row, src_row, coef_t, rel_emb, basis = places
+    mix, counts, degree_inv, rel_images = results
+    edges, rows = target.shape
+    width = rel_emb.shape[1]
     blocks, relations = coef_t.shape
     live_edges = tile_count[0, 0] * TILE
     size = 256
@@ -134,12 +132,9 @@
     )
     copies[3].wait()
     edge_coef[...] = dot(coef_t[...].astype(BF), rel_hot)
-    counts[...] = dot(rel_hot, target[...]).astype(BF)
-    degree = 1.0 + dot(jnp.ones((8, edges), BF), target[...])
-    degree_inv[...] = spread_column((1.0 / degree)[:1])
-    stores = fetched((counts, degree_inv), outs[1:3], out_sems, 0)
     copies[2].wait()
     part = min(256, slots)
+    stores = []
     for b in range(blocks):
 
         @tiles(slots, part)
@@ -154,7 +149,12 @@
                 weighted, target[...]
             ).astype(BF)
 
-    stores += fetched((mix,), outs[:1], out_sems, 2)
+        lines = pl.ds(b * slots, slots)
+        stores += fetched((mix.at[lines],), (outs[0].at[lines],), out_sems, b)
+    counts[...] = dot(rel_hot, target[...]).astype(BF)
+    degree = 1.0 + dot(jnp.ones((8, edges), BF), target[...])
+    degree_inv[...] = spread_column((1.0 / degree)[:1])
+    stores += fetched((counts, degree_inv), outs[1:3], out_sems, blocks)
     copies[4].wait()
     copies[5].wait()
     folded = jnp.zeros((relations, width), F32)
@@ -162,44 +162,24 @@
         scale = lane_tiled(spread_column(coef_t[b : b + 1, :]), width)
         folded += scale * dot(rel_emb[...], basis[:, b * width : (b + 1) * width])
     rel_images[...] = folded.astype(BF)
-    for copy in copies[6:]:
-        copy.wait()
-
-    @tiles(rows, 256)
-    def _(block, i):
-        own = states[block, :]
-        partial[block, :] = dot(own, self_weight[...]) + dot(
-            counts[:, block], rel_images[...], 0, 0
-        )
-        gate[block, :] = lax.logistic(dot(own, gate_weight[...]) + gate_bias[...])
-
-    stores += fetched((partial, gate), outs[3:], out_sems, 3)
+    stores += fetched((rel_images,), outs[3:], out_sems, blocks + 2)
     for copy in stores:
         copy.wait()
 
 
 def forward_kernel(slots, *refs):
-    received = refs[0]
-    sources = refs[1:10]
-    basis, mix, gate, self_weight, gate_weight, cotangent = refs[10:16]
-    alpha, beta, row_grad, dense, images_any = refs[16:21]
-    partial, degree_inv, states, images, sems = refs[21:]
-    places = (
-        basis,
-        mix,
-        degree_inv,
-        partial,
-        gate,
-        states,
-        cotangent,
-        self_weight,
-        gate_weight,
-    )
+    sources, outs = refs[:11], refs[11:17]
+    places, results = refs[17:28], refs[28:34]
+    in_sems, tile_sems, store_sem = refs[34:]
+    received, basis, mix, self_weight, gate_weight, gate_bias = places[:6]
+    counts, rel_images, degree_inv, states, cotangent = places[6:]
+    dense, row_grad, gate, alpha, beta, images = results
     rows, width = states.shape
     blocks = basis.shape[1] // width
     part = min(256, slots)
-    copies = fetched(sources, places, sems)
+    copies = fetched(sources, places, in_sems)
     copies[0].wait()
+    copies[1].wait()
     for b in range(blocks):
 
         @tiles(slots, part)
@@ -208,21 +188,31 @@
                 received[block, :], basis[:, b * width : (b + 1) * width]
             ).astype(BF)
 
-    store = pltpu.make_async_copy(images, images_any, sems.at[9])
+    store = pltpu.make_async_copy(images, outs[5], store_sem)
     store.start()
-    for copy in copies[1:]:
+    for copy in copies[2:]:
         copy.wait()
+
+    def tile_copies(block, i):
+        return [
+            pltpu.make_async_copy(results[k].at[block], outs[k].at[block], tile_sems.at[k, i])
+            for k in range(5)
+        ]
 
     @tiles(rows, 256)
     def _(block, i):
+        own = states[block, :]
         scale = lane_tiled(degree_inv[block, :], width)
-        summed = (dot(mix[:, block], images[...], 0, 0) + partial[block, :]) * scale
+        summed = (
+            dot(mix[:, block], images[...], 0, 0)
+            + dot(counts[:, block], rel_images[...], 0, 0)
+            + dot(own, self_weight[...])
+        ) * scale
         aggregated = jnp.tanh(summed)
-        opened = gate[block, :]
+        opened = lax.logistic(dot(own, gate_weight[...]) + gate_bias[...])
         row_scale = opened * (1.0 - aggregated * aggregated) * scale
-        gate_scale = (
-            (aggregated - states[block, :].astype(F32)) * opened * (1.0 - opened)
-        )
+        gate_scale = (aggregated - own.astype(F32)) * opened * (1.0 - opened)
+        gate[block, :] = opened
         alpha[block, :] = row_scale
         beta[block, :] = gate_scale
         upstream = cotangent[block, :].astype(F32)
@@ -234,6 +224,13 @@
             + dot((upstream * gate_scale).astype(BF), gate_weight[...], 1, 1)
         )
         dense[block, :] = value.astype(dense.dtype)
+        for copy in tile_copies(block, i):
+            copy.start()
+
+    @tiles(rows, 256)
+    def _(block, i):
+        for copy in tile_copies(block, i):
+            copy.wait()
 
     store.wait()
 
@@ -364,10 +361,41 @@
     slots,
     parts,
     order,
+    received,
+    mixed,
+    coef_t,
+    rel_emb,
+    rel_sum,
+    kept,
+    sent,
+    scaled,
+    total,
+):
+    width = received.shape[1]
+    cut = width // parts
+    place = placer(parts, order)
+    for b in range(1, coef_t.shape[0]):
+        lines = mixed[b * slots : (b + 1) * slots, :]
+        total[...] = basis_term(
+            b, slots, received, lines, coef_t, rel_sum, rel_emb, scaled
+        )
+        for i in range(0, parts, 2):
+            place(
+                i,
+                kept,
+                sent,
+                (b - 1) * cut,
+                total[i * cut : (i + 1) * cut, :],
+                total[(i + 1) * cut : (i + 2) * cut, :],
+            )
+
+
+def third_weight_kernel(
+    slots,
+    parts,
     tile_count,
     row_grad,
-    received,
-    mixed,
+    slot_grad,
     coef_t,
     rel_emb,
     basis,
@@ -377,10 +405,8 @@
     src_row,
     dst_row,
     rel_row,
-    kept,
-    sent,
+    packed,
     scaled,
-    total,
     edge_grad,
 ):
     rows, width = row_grad.shape
@@ -389,7 +415,9 @@
     cut = width // parts
     rel_cut = relations // parts
     rel_room = rounded_up(rel_cut, 16)
-    place = placer(parts, order)
+    per_owner = slots // parts
+    for p in range(parts):
+        packed[p, :per_owner, :] = slot_grad[p * per_owner : (p + 1) * per_owner, :]
     rel_grad = jnp.zeros((relations, width), F32)
     corner = []
     for b in range(blocks):
@@ -401,31 +429,9 @@
                 keepdims=True,
             )
         )
-        term = basis_term(
-            b,
-            slots,
-            received,
-            mixed[b * slots : (b + 1) * slots, :],
-            coef_t,
-            rel_sum,
-            rel_emb,
-            scaled,
-        ) if b else None
-        if not b:
-            scale = lane_tiled(spread_column(coef_t[:1, :]), width)
-            scaled[...] = (scale * rel_sum[...]).astype(BF)
+        scale = lane_tiled(spread_column(coef_t[b : b + 1, :]), width)
+        scaled[...] = (scale * rel_sum[...]).astype(BF)
         rel_grad += dot(scaled[...], basis[:, columns], 1, 1)
-        if b:
-            total[...] = term
-            for i in range(0, parts, 2):
-                place(
-                    i,
-                    kept,
-                    sent,
-                    (b - 1) * cut,
-                    total[i * cut : (i + 1) * cut, :],
-                    total[(i + 1) * cut : (i + 2) * cut, :],
-                )
 
     size = 256
     live_edges = tile_count[0, 0] * TILE
@@ -466,21 +472,13 @@
             [turned, jnp.zeros((8, width - relations), F32)], axis=1
         )
     bias8 = jnp.broadcast_to(bias[...], (8, width))
-    at = (blocks - 1) * cut
-    rest = kept.shape[1] - at - rel_room
-
-    def last_rows(p):
+    for p in range(parts):
         lines = [rel_grad[p * rel_cut : (p + 1) * rel_cut]]
         if rel_room > rel_cut:
             lines.append(jnp.zeros((rel_room - rel_cut, width), F32))
         lines.append(turned if p == 0 else pltpu.roll(turned, width - p * rel_cut, 1))
         lines.append(bias8 if p == 0 else pltpu.roll(bias8, width - p * cut, 1))
-        if rest > 16:
-            lines.append(jnp.zeros((rest - 16, width), F32))
-        return jnp.concatenate(lines, axis=0)
-
-    for i in range(0, parts, 2):
-        place(i, kept, sent, at, last_rows(i), last_rows(i + 1))
+        packed[p, per_owner:, :] = jnp.concatenate(lines, axis=0).astype(BF)
 
 
 def fold_kernel(kept, taken, next_kept, next_sent):
@@ -491,13 +489,20 @@
         next_sent[spot] = (kept[other].astype(F32) + taken[other].astype(F32)).astype(BF)
 
 
-def join_kernel(kept_a, taken_a, kept_b, taken_b, joined):
+def join_kernel(per_owner, kept_a, taken_a, kept_b, taken_b, packed, joined):
+    size, width = joined.shape[1:]
+    rest = packed[0, per_owner:, :].astype(F32)
+    for k in range(1, packed.shape[0]):
+        rest += packed[k, per_owner:, :].astype(F32)
     parts = [
         kept_a[0].astype(F32) + taken_a[0].astype(F32),
         kept_b[0].astype(F32) + taken_b[0].astype(F32),
+        rest,
     ]
+    unused = size * joined.shape[0] - sum(part.shape[0] for part in parts)
+    if unused:
+        parts.append(jnp.zeros((unused, width), F32))
     whole = jnp.concatenate(parts, axis=0).astype(BF)
-    size = joined.shape[1]
     for k in range(joined.shape[0]):
         joined[k] = whole[k * size : (k + 1) * size]
 
@@ -524,10 +529,14 @@
     bias[...] = value[at + 8 : at + 9, :cut]
 
 
-def output_kernel(dense, returned, export_row, total):
+def output_kernel(dense, packed, export_row, total, returned):
     rows = dense.shape[0]
     slots = export_row.shape[1]
+    parts = packed.shape[0]
+    per_owner = slots // parts
     size = 256
+    for p in range(parts):
+        returned[p * per_owner : (p + 1) * per_owner, :] = packed[p, :per_owner, :]
 
     @tiles(rows, size)
     def _(block, i):
@@ -583,33 +592,21 @@
             VM((slots, width), BF),
             dma((3,)),
         ),
-        flops=2 * slots * rows * width,
+        flops=LIGHT,
         limit=FULL,
     )
     received = exchange(sent)
     export_next = from_next(export_rows, "tm")
     coef_t = coef.T
     bias_row = gate_bias[None]
-    sources = [
-        edge_dst,
-        edge_rel,
-        edge_src,
-        coef_t,
-        rel_emb,
-        basis,
-        own,
-        self_weight,
-        gate_weight,
-        bias_row,
-    ]
+    sources = [edge_dst, edge_rel, edge_src, coef_t, rel_emb, basis]
     made = [
         ((blocks * slots, rows), BF),
         ((relations, rows), BF),
         ((rows, LANES), F32),
-        ((rows, width), F32),
-        ((rows, width), F32),
+        ((relations, width), BF),
     ]
-    mix, counts, degree_inv, partial, gate = call(
+    mix, counts, degree_inv, rel_images = call(
         functools.partial(setup_kernel, slots),
         [out + (ANY,) for out in made],
         [(tile_count, pltpu.SMEM)] + [(array, ANY) for array in sources],
@@ -618,62 +615,50 @@
         + [
             VM((edges, rows), BF),
             VM((blocks, edges), F32),
-            VM((relations, width), BF),
             dma((len(sources),)),
-            dma((len(made),)),
+            dma((blocks + 3,)),
         ],
-        flops=2 * blocks * slots * rows * edges,
+        flops=LIGHT,
         limit=FULL,
     )
-    outs = call(
+    sources = [
+        received,
+        basis,
+        mix,
+        self_weight,
+        gate_weight,
+        bias_row,
+        counts,
+        rel_images,
+        degree_inv,
+        own,
+        cot,
+    ]
+    made = [
+        ((rows, width), BF),
+        ((rows, width), BF),
+        ((rows, width), F32),
+        ((rows, width), F32),
+        ((rows, width), F32),
+        ((blocks * slots, width), BF),
+    ]
+    dense, row_grad, gate, alpha, beta, images = call(
         functools.partial(forward_kernel, slots),
-        [
-            (basis.shape, BF, VM),
-            (mix.shape, BF, VM),
-            ((rows, width), F32, VM),
-            ((width, width), BF, VM),
-            ((width, width), BF, VM),
-            ((rows, width), BF, VM),
-            ((rows, width), F32, VM),
-            ((rows, width), F32, VM),
-            ((rows, width), BF, VM),
-            ((rows, width), BF, VM),
-            ((blocks * slots, width), BF, ANY),
-        ],
-        [(received, VM)]
-        + [
-            (array, ANY)
-            for array in (
-                basis,
-                mix,
-                degree_inv,
-                partial,
-                gate,
-                own,
-                cot,
-                self_weight,
-                gate_weight,
-            )
-        ],
-        scratch=[
-            VM((rows, width), F32),
-            VM((rows, LANES), F32),
-            VM((rows, width), BF),
-            VM((blocks * slots, width), BF),
-            dma((10,)),
-        ],
-        flops=4 * blocks * slots * rows * width,
-        limit=FULL - (16 << 20),
-    )
-    basis_near, mix_near, gate_near, self_near, gate_weight_near, cot_near = outs[:6]
-    alpha, beta, row_grad, dense, images = outs[6:]
+        [out + (ANY,) for out in made],
+        [(array, ANY) for array in sources],
+        scratch=[VM(array.shape, array.dtype) for array in sources]
+        + [VM(dims, kind) for dims, kind in made]
+        + [dma((len(sources),)), dma((5, max(rows // 256, 1))), dma],
+        flops=LIGHT,
+        limit=FULL,
+    )
 
     def slot_step(row_grad):
         return call(
             functools.partial(slot_kernel, slots),
             [((slots, width), BF, VM), ((blocks * slots, width), BF, VM)],
-            [(row_grad, VM), (mix_near, VM), (basis_near, VM)],
-            flops=4 * blocks * slots * rows * width,
+            [(row_grad, VM), (mix, VM), (basis, VM)],
+            flops=LIGHT,
         )
 
     for step in range(1, section_count):
@@ -681,7 +666,7 @@
         slot_grad, _ = slot_step(row_grad)
         ahead = from_next(dense, "tm")
         returned = from_next(exchange(slot_grad), "tm")
-        args = [cot_near, alpha, beta, gate_near, self_near, gate_weight_near]
+        args = [cot, alpha, beta, gate, self_weight, gate_weight]
         args += [ahead, returned, export_next]
         outs = [((rows, width), BF, VM), ((rows, width), F32 if last else BF, VM)]
         if last:
@@ -690,15 +675,16 @@
             functools.partial(dense_kernel, last),
             outs,
             [(array, VM) for array in args],
-            flops=4 * rows * width * width,
+            flops=LIGHT,
         )
         row_grad, dense = outs[:2]
     gate_row, bias = outs[2:]
 
     cut, rel_cut = width // ent_count, relations // ent_count
     first_depth = 3 * cut
-    rest = (blocks - 1) * cut + rounded_up(rel_cut, 16) + 16
-    depth = rounded_up(first_depth + rest, 16 * section_count)
+    second_depth = (blocks - 1) * cut
+    third_depth = rounded_up(rel_cut, 16) + 16
+    depth = rounded_up(first_depth + second_depth + third_depth, 16 * section_count)
     distances = []
     while 1 << len(distances) < ent_count:
         distances.append(1 << len(distances))
@@ -718,29 +704,35 @@
                 gate_row,
                 own,
                 received,
-                mix_near,
+                mix,
                 counts,
                 coef_t,
                 rel_emb,
             )
         ],
         scratch=[VM((relations, width), BF), VM((width, width), F32)],
-        flops=4 * rows * width * width,
+        flops=LIGHT,
     )
     slot_grad, mixed = slot_step(row_grad)
     kept_b, sent_b = call(
         functools.partial(second_weight_kernel, slots, ent_count, orders[1]),
-        [((half, depth - first_depth, width), BF, VM)] * 2,
+        [((half, second_depth, width), BF, VM)] * 2,
+        [(array, VM) for array in (received, mixed, coef_t, rel_emb, rel_sum)],
+        scratch=[VM((relations, width), BF), VM((width, width), F32)],
+        flops=LIGHT,
+    )
+    packed = call(
+        functools.partial(third_weight_kernel, slots, ent_count),
+        ((ent_count, per_owner + third_depth, width), BF, VM),
         [(tile_count, pltpu.SMEM)]
         + [
             (array, VM)
             for array in (
                 row_grad,
-                received,
-                mixed,
+                slot_grad,
                 coef_t,
                 rel_emb,
-                basis_near,
+                basis,
                 bias,
                 images,
                 rel_sum,
@@ -749,13 +741,10 @@
                 edge_rel,
             )
         ],
-        scratch=[
-            VM((relations, width), BF),
-            VM((width, width), F32),
-            VM((256, width), BF),
-        ],
-        flops=8 * blocks * slots * rows * width,
-    )
+        scratch=[VM((relations, width), BF), VM((256, width), BF)],
+        flops=LIGHT,
+    )
+    packed = lax.all_to_all(packed, "ent", 0, 0, tiled=True)
     folds = [(kept_a, sent_a), (kept_b, sent_b)]
     taken = [None, None]
     for k in range(len(distances)):
@@ -772,26 +761,27 @@
                     fold_kernel,
                     [(dims, BF, VM)] * 2,
                     [(kept, VM), (taken[which], VM)],
-                    flops=1 << 20,
+                    flops=LIGHT,
                 )
     joined = call(
-        join_kernel,
+        functools.partial(join_kernel, per_owner),
         ((section_count, depth // section_count, width), BF, VM),
-        [(folds[0][0], VM), (taken[0], VM), (folds[1][0], VM), (taken[1], VM)],
-        flops=1 << 20,
-    )
-    returned = exchange(slot_grad)
+        [(folds[0][0], VM), (taken[0], VM), (folds[1][0], VM), (taken[1], VM)]
+        + [(packed, VM)],
+        flops=LIGHT,
+    )
     state_grad = call(
         output_kernel,
         ((rows, width), F32, VM),
-        [(dense, VM), (returned, VM), (export_rows, VM)],
-        flops=2 * rows * slots * width,
+        [(dense, VM), (packed, VM), (export_rows, VM)],
+        scratch=[VM((slots, width), BF)],
+        flops=LIGHT,
     )
     quarter = call(
         quarter_kernel,
         ((depth // section_count, width), BF, VM),
         [(lax.all_to_all(joined, "tm", 0, 0, tiled=True), VM)],
-        flops=1 << 20,
+        flops=LIGHT,
     )
     final = lax.all_gather(quarter, "tm", axis=0, tiled=True)
     grad_basis, grad_self, grad_gate, grad_rel, grad_coef, grad_bias = call(
@@ -805,7 +795,7 @@
             ((1, cut), F32, VM),
         ],
         [(final, VM)],
-        flops=1 << 20,
+        flops=LIGHT,
     )
     return (
         state_grad[None],

time: 217 us -> 207 us (0.954)
  waiting for transfers between devices: 75.8 us -> 62.5 us
  local copies, waits for them, and re-layouts: 5.32 us -> 12.2 us
  Pallas kernels: 58.7 us -> 54.4 us
    ppermute x6, waiting for transfers between devices: 21 us -> 5.24 us  [per_device(): taken[which] = lax.ppermute(moved, 'ent', route)]
    unnamed x34 -> x60, local copies, waits for them, and re-layouts: 5.32 us -> 12.2 us
    pallas_call x20 -> x21, Pallas kernels: 58.7 us -> 54.4 us  [call(): pl.pallas_call(kernel, out_shape=out_shape[0] if single else out_shape, i...]
    all_to_all x0 -> x1, starting transfers between devices: none -> 3.54 us  [per_device(): packed = lax.all_to_all(packed, 'ent', 0, 0, tiled=True)]
    all_to_all x2 -> x1, starting transfers between devices: 8.62 us -> 5.21 us  [exchange(): lax.all_to_all(block.reshape(ent_count, per_owner, width), 'ent', 0, 0, t...]
    all_to_all x0 -> x1, waiting for transfers between devices: none -> 3.29 us  [per_device(): packed = lax.all_to_all(packed, 'ent', 0, 0, tiled=True)]
  transfers between devices with their start and end apart: 16 -> 16, of which waited for: 7 -> 8; matrix products, arithmetic and copies ran while one was open for 0% -> 0% of each run, Pallas kernels for 11% -> 13%
where the time goes in v3:
time: 207 us; the launch traced here: 206 us
  waiting for transfers between devices  62.5 us (30%)
  Pallas kernels  54.4 us (26%)
  blocking collectives  46.9 us (23%)
  starting transfers between devices  28.2 us (14%)
  local copies, waits for them, and re-layouts  12.2 us (6%)
    pallas_call x21, Pallas kernels, call(): pl.pallas_call(kernel, out_shape=out_shape[0] if single else out_shape, i...  54.4 us
    ppermute x7, waiting for transfers between devices, from_next(): return lax.ppermute(block, axis, [(i, i - 1) for i in range(1, count)])  43.1 us
    all_to_all x3, blocking collectives, exchange(): lax.all_to_all(block.reshape(ent_count, per_owner, width), 'ent', 0, 0, t...  31.5 us
    all_gather x1, blocking collectives, per_device(): final = lax.all_gather(quarter, 'tm', axis=0, tiled=True)  15.4 us
    unnamed x60, local copies, waits for them, and re-layouts  12.2 us
    all_to_all x1, waiting for transfers between devices, per_device(): lax.all_to_all(joined, 'tm', 0, 0, tiled=True)  10.8 us
    ppermute x7, starting transfers between devices, from_next(): return lax.ppermute(block, axis, [(i, i - 1) for i in range(1, count)])  9.19 us
    ppermute x6, starting transfers between devices, per_device(): taken[which] = lax.ppermute(moved, 'ent', route)  6.38 us
  transfers between devices with their start and end apart: 16, of which 8 were waited for; matrix products, arithmetic and copies ran while one was open for 0% of the time, Pallas kernels for 13%

profile of v3, /device:TPU:0, one launch (start us, length us, event | category | flops | bytes accessed | tf_op | source)
XLA Modules:
  0.0 205.9 jit_solution(11084569509887324079)
XLA Ops:
  0.6 2.5 %shard_map.180 = bf16[256,512]{1,0:T(8,128)(2,1)} custom-call(bf16[1024,512]{1,0:T(8,128)(2,1)} %bitcast.19, s32[1,256]{1,0:T(1,128)} %export_row.1), custom_call_target="tpu_custom_call" | custom-call | flops 1048576 | bytes 4194304 | tf_op jit(solution)/shard_map/pallas_call | solution.py:49
  3.1 5.2 %all-to-all-start = ((bf16[8,32,512]{2,1,0:T(8,128)(2,1)}), bf16[8,32,512]{2,1,0:T(8,128)(2,1)S(1)}, u32[]{:S(2)}, u32[]{:S(2)}) async-start(bf16[8,32,512]{2,1,0:T(8,128)(2,1)} %bitcast.33), calls=%async_computation | async-start | bytes 524288 | tf_op jit(solution)/shard_map/all_to_all | solution.py:580
  9.0 6.5 %shard_map.181 = (bf16[1024,1024]{1,0:T(8,128)(2,1)}, bf16[256,1024]{1,0:T(8,128)(2,1)}, f32[1024,128]{1,0:T(8,128)}, bf16[256,512]{1,0:T(8,128)(2,1)}) custom-call(s32[1,1]{1,0:T(1,128)S(6)} %copy.20.refs_0_.tile_count, s32[1,1024]{1,0:T(1,128)} %dst_row.1, s32[1,1024]{1,0:T(1,128)} %rel_row.1, s32[1,1024]{1,0:T(1,128)} %src_row.1, f32[4,256]{1,0:T(4,128)} %bitcast.28, ...), custom_call_target="tpu_custom_call" | custom-call | flops 1048576 | bytes 4194304 | tf_op jit(solution)/shard_map/pallas_call | solution.py:49
  16.2 11.0 %shard_map.182 = (bf16[1024,512]{1,0:T(8,128)(2,1)}, bf16[1024,512]{1,0:T(8,128)(2,1)}, f32[1024,512]{1,0:T(8,128)}, f32[1024,512]{1,0:T(8,128)}, f32[1024,512]{1,0:T(8,128)}, /*index=5*/bf16[1024,512]{1,0:T(8,128)(2,1)}) custom-call(bf16[256,512]{1,0:T(8,128)(2,1)} %bitcast.22, bf16[512,2048]{1,0:T(8,128)(2,1)} %basis.9, ...), custom_call_target="tpu_custom_call" | custom-call | flops 1048576 | bytes 4194304 | tf_op jit(solution)/shard_map/pallas_call | solution.py:49
  32.9 2.8 %shard_map.183 = (bf16[256,512]{1,0:T(8,128)(2,1)S(1)}, bf16[1024,512]{1,0:T(8,128)(2,1)}) custom-call(bf16[1024,512]{1,0:T(8,128)(2,1)S(1)} %copy-done.19, bf16[1024,1024]{1,0:T(8,128)(2,1)S(1)} %copy-done.2, bf16[512,2048]{1,0:T(8,128)(2,1)S(1)} %copy-done), custom_call_target="tpu_custom_call" | custom-call | flops 1048576 | bytes 4194304 | tf_op jit(solution)/shard_map/pallas_call | solution.py:49
  35.7 10.9 %all_to_all.30 = bf16[8,32,512]{2,1,0:T(8,128)(2,1)S(1)} all-to-all(bf16[8,32,512]{2,1,0:T(8,128)(2,1)S(1)} %bitcast.25), channel_id=1, replica_groups=mesh['tm'=4,'ent'=8] {'ent'}, dimensions={0} | all-to-all | bytes 524288 | tf_op jit(solution)/shard_map/all_to_all | solution.py:580
  49.2 11.3 %collective-permute-done.2.refs_8_ = s32[1,256]{1,0:T(1,128)S(1)} collective-permute-done((s32[1,256]{1,0:T(1,128)S(1)}, s32[1,256]{1,0:T(1,128)S(1)}, u32[]{:S(2)}, u32[]{:S(2)}) %collective-permute-start.2) | collective-permute-done | bytes 1056 | tf_op jit(solution)/shard_map/ppermute | solution.py:550
  62.2 2.3 %shard_map.184 = (bf16[1024,512]{1,0:T(8,128)(2,1)S(1)}, bf16[1024,512]{1,0:T(8,128)(2,1)S(1)}) custom-call(bf16[1024,512]{1,0:T(8,128)(2,1)S(1)} %bitcast.16, f32[1024,512]{1,0:T(8,128)S(1)} %copy-done.5, f32[1024,512]{1,0:T(8,128)S(1)} %copy-done.6, f32[1024,512]{1,0:T(8,128)S(1)} %copy-done.4, bf16[512,512]{1,0:T(8,128)(2,1)S(1)} %copy-done.10, ...), custom_call_target="tpu_custom_call" | custom-call | flops 1048576 | bytes 4194304 | tf_op jit(solution)/shard_map/pallas_call | solution.py:49
  65.8 2.8 %shard_map.185 = (bf16[256,512]{1,0:T(8,128)(2,1)S(1)}, bf16[1024,512]{1,0:T(8,128)(2,1)}) custom-call(bf16[1024,512]{1,0:T(8,128)(2,1)S(1)} %get-tuple-element.60.row_grad, bf16[1024,1024]{1,0:T(8,128)(2,1)S(1)} %copy-done.3, bf16[512,2048]{1,0:T(8,128)(2,1)S(1)} %copy-done.1), custom_call_target="tpu_custom_call" | custom-call | flops 1048576 | bytes 4194304 | tf_op jit(solution)/shard_map/pallas_call | solution.py:49
  68.6 10.5 %all_to_all.31 = bf16[8,32,512]{2,1,0:T(8,128)(2,1)S(1)} all-to-all(bf16[8,32,512]{2,1,0:T(8,128)(2,1)S(1)} %bitcast.26), channel_id=1, replica_groups=mesh['tm'=4,'ent'=8] {'ent'}, dimensions={0} | all-to-all | bytes 524288 | tf_op jit(solution)/shard_map/all_to_all | solution.py:580
  80.4 16.2 %collective-permute-done.4.refs_7_ = bf16[256,512]{1,0:T(8,128)(2,1)S(1)} collective-permute-done((bf16[256,512]{1,0:T(8,128)(2,1)S(1)}, bf16[256,512]{1,0:T(8,128)(2,1)S(1)}, u32[]{:S(2)}, u32[]{:S(2)}) %collective-permute-start.4) | collective-permute-done | bytes 262176 | tf_op jit(solution)/shard_map/ppermute | solution.py:550
  96.7 2.3 %shard_map.186 = (bf16[1024,512]{1,0:T(8,128)(2,1)S(1)}, bf16[1024,512]{1,0:T(8,128)(2,1)S(1)}) custom-call(bf16[1024,512]{1,0:T(8,128)(2,1)S(1)} %bitcast.17, f32[1024,512]{1,0:T(8,128)S(1)} %copy-done.5, f32[1024,512]{1,0:T(8,128)S(1)} %copy-done.6, f32[1024,512]{1,0:T(8,128)S(1)} %copy-done.4, bf16[512,512]{1,0:T(8,128)(2,1)S(1)} %copy-done.10, ...), custom_call_target="tpu_custom_call" | custom-call | flops 1048576 | bytes 4194304 | tf_op jit(solution)/shard_map/pallas_call | solution.py:49
  100.4 2.9 %shard_map.187 = (bf16[256,512]{1,0:T(8,128)(2,1)S(1)}, bf16[1024,512]{1,0:T(8,128)(2,1)}) custom-call(bf16[1024,512]{1,0:T(8,128)(2,1)S(1)} %get-tuple-element.63.row_grad, bf16[1024,1024]{1,0:T(8,128)(2,1)S(1)} %copy-done.3, bf16[512,2048]{1,0:T(8,128)(2,1)S(1)} %copy-done.1), custom_call_target="tpu_custom_call" | custom-call | flops 1048576 | bytes 4194304 | tf_op jit(solution)/shard_map/pallas_call | solution.py:49
  103.3 10.1 %all_to_all.32 = bf16[8,32,512]{2,1,0:T(8,128)(2,1)S(1)} all-to-all(bf16[8,32,512]{2,1,0:T(8,128)(2,1)S(1)} %bitcast.27), channel_id=1, replica_groups=mesh['tm'=4,'ent'=8] {'ent'}, dimensions={0} | all-to-all | bytes 524288 | tf_op jit(solution)/shard_map/all_to_all | solution.py:580
  114.7 15.6 %collective-permute-done.6.refs_7_ = bf16[256,512]{1,0:T(8,128)(2,1)S(1)} collective-permute-done((bf16[256,512]{1,0:T(8,128)(2,1)S(1)}, bf16[256,512]{1,0:T(8,128)(2,1)S(1)}, u32[]{:S(2)}, u32[]{:S(2)}) %collective-permute-start.6) | collective-permute-done | bytes 262176 | tf_op jit(solution)/shard_map/ppermute | solution.py:550
  130.3 2.6 %shard_map.188 = (bf16[1024,512]{1,0:T(8,128)(2,1)S(1)}, f32[1024,512]{1,0:T(8,128)S(1)}, bf16[1024,512]{1,0:T(8,128)(2,1)S(1)}, f32[1,512]{1,0:T(1,128)S(1)}) custom-call(bf16[1024,512]{1,0:T(8,128)(2,1)S(1)} %bitcast.18, f32[1024,512]{1,0:T(8,128)S(1)} %copy-done.5, f32[1024,512]{1,0:T(8,128)S(1)} %copy-done.7, f32[1024,512]{1,0:T(8,128)S(1)} %copy-done.4, ...), custom_call_target="tpu_custom_call" | custom-call | flops 1048576 | bytes 4194304 | tf_op jit(solution)/shard_map/pallas_call | solution.py:49
  145.3 6.7 %shard_map.191 = bf16[8,80,512]{2,1,0:T(8,128)(2,1)} custom-call(s32[1,1]{1,0:T(1,128)S(6)} %copy.20.refs_0_.tile_count, bf16[1024,512]{1,0:T(8,128)(2,1)S(1)} %get-tuple-element.66.row_grad, bf16[256,512]{1,0:T(8,128)(2,1)S(1)} %get-tuple-element.67.slot_grad, f32[4,256]{1,0:T(4,128)S(1)} %bitcast.31, bf16[256,512]{1,0:T(8,128)(2,1)S(1)} %copy-done.14, ...), custom_call_target="tpu_custom_call" | custom-call | flops 1048576 | bytes 4194304 | tf_op jit(solution)/shard_map/pallas_call | solution.py:49
  152.1 3.5 %all-to-all-start.4 = ((bf16[8,80,512]{2,1,0:T(8,128)(2,1)}), bf16[8,80,512]{2,1,0:T(8,128)(2,1)S(1)}, u32[]{:S(2)}, u32[]{:S(2)}) async-start(bf16[8,80,512]{2,1,0:T(8,128)(2,1)} %shard_map.191), calls=%async_computation.4 | async-start | bytes 1310720 | tf_op jit(solution)/shard_map/all_to_all | solution.py:747
  164.0 3.3 %all-to-all-done.4.packed = bf16[8,80,512]{2,1,0:T(8,128)(2,1)S(1)} async-done(((bf16[8,80,512]{2,1,0:T(8,128)(2,1)}), bf16[8,80,512]{2,1,0:T(8,128)(2,1)S(1)}, u32[]{:S(2)}, u32[]{:S(2)}) %all-to-all-start.4) | async-done | bytes 655392 | tf_op jit(solution)/shard_map/all_to_all | solution.py:747
  167.3 2.7 %collective-permute-done.12.taken_b = bf16[1,192,512]{2,1,0:T(8,128)(2,1)S(1)} collective-permute-done((bf16[1,192,512]{2,1,0:T(8,128)(2,1)}, bf16[1,192,512]{2,1,0:T(8,128)(2,1)S(1)}, u32[]{:S(2)}, u32[]{:S(2)}) %collective-permute-start.12) | collective-permute-done | bytes 196640 | tf_op jit(solution)/shard_map/ppermute | solution.py:755
  172.6 3.9 %all-to-all-start.5 = ((bf16[4,112,512]{2,1,0:T(8,128)(2,1)}), bf16[4,112,512]{2,1,0:T(8,128)(2,1)S(1)}, u32[]{:S(2)}, u32[]{:S(2)}) async-start(bf16[4,112,512]{2,1,0:T(8,128)(2,1)} %copy-done.18), calls=%async_computation.5 | async-start | bytes 917504 | tf_op jit(solution)/shard_map/all_to_all | solution.py:783
  176.4 2.2 %shard_map.192 = f32[1024,512]{1,0:T(8,128)} custom-call(f32[1024,512]{1,0:T(8,128)S(1)} %copy-done.16, bf16[8,80,512]{2,1,0:T(8,128)(2,1)S(1)} %all-to-all-done.4.packed, s32[1,256]{1,0:T(1,128)S(1)} %copy-done.29), custom_call_target="tpu_custom_call" | custom-call | flops 1048576 | bytes 4194304 | tf_op jit(solution)/shard_map/pallas_call | solution.py:49
  178.7 10.8 %all-to-all-done.5.taken = bf16[4,112,512]{2,1,0:T(8,128)(2,1)S(1)} async-done(((bf16[4,112,512]{2,1,0:T(8,128)(2,1)}), bf16[4,112,512]{2,1,0:T(8,128)(2,1)S(1)}, u32[]{:S(2)}, u32[]{:S(2)}) %all-to-all-start.5) | async-done | bytes 458784 | tf_op jit(solution)/shard_map/all_to_all | solution.py:783
  189.6 15.4 %all_gather.3.final = bf16[448,512]{1,0:T(8,128)(2,1)S(1)} all-gather(bf16[112,512]{1,0:T(8,128)(2,1)S(1)} %shard_map.199), channel_id=1, replica_groups=mesh['tm'=4,'ent'=8] {'tm'}, dimensions={0}, use_global_device_ids=true | all-gather | bytes 573440 | tf_op jit(solution)/shard_map/all_gather | solution.py:786
  (93 shorter events, 40.1 us)
Async XLA Ops:
  3.1 12.3 %all-to-all-start = ((bf16[8,32,512]{2,1,0:T(8,128)(2,1)}), bf16[8,32,512]{2,1,0:T(8,128)(2,1)S(1)}, u32[]{:S(2)}, u32[]{:S(2)}) async-start(bf16[8,32,512]{2,1,0:T(8,128)(2,1)} %bitcast.33), calls=%async_computation | async-start | bytes 524288 | tf_op jit(solution)/shard_map/all_to_all | solution.py:580
  16.2 44.4 %copy-start.11 = (bf16[512,512]{1,0:T(8,128)(2,1)S(1)}, bf16[512,512]{1,0:T(8,128)(2,1)}, u32[]{:S(2)}) copy-start(bf16[512,512]{1,0:T(8,128)(2,1)} %refs_5_.7) | copy-start | bytes 1572868
  27.2 33.4 %collective-permute-start = (bf16[1024,512]{1,0:T(8,128)(2,1)}, bf16[1024,512]{1,0:T(8,128)(2,1)S(1)}, u32[]{:S(2)}, u32[]{:S(2)}) collective-permute-start(bf16[1024,512]{1,0:T(8,128)(2,1)} %get-tuple-element.56), channel_id=1, source_target_pairs={{8,0},{16,8},{24,16},{9,1},{17,9},{25,17},{10,2},{18,10},{26,18},{... | collective-permute-start | bytes 3145736 | tf_op jit(solution)/shard_map/ppermute | solution.py:550
  32.9 15.0 %copy-start.29 = (s32[1,256]{1,0:T(1,128)S(1)}, s32[1,256]{1,0:T(1,128)}, u32[]{:S(2)}) copy-start(s32[1,256]{1,0:T(1,128)} %export_row.1) | copy-start | bytes 3076
  32.9 27.7 %copy-start.4 = (f32[1024,512]{1,0:T(8,128)S(1)}, f32[1024,512]{1,0:T(8,128)}, u32[]{:S(2)}) copy-start(f32[1024,512]{1,0:T(8,128)} %get-tuple-element.55.refs_3_) | copy-start | bytes 6291460
  32.9 27.7 %copy-start.5 = (f32[1024,512]{1,0:T(8,128)S(1)}, f32[1024,512]{1,0:T(8,128)}, u32[]{:S(2)}) copy-start(f32[1024,512]{1,0:T(8,128)} %get-tuple-element.53.refs_1_) | copy-start | bytes 6291460
  32.9 27.7 %copy-start.8 = (bf16[1,1024,512]{2,1,0:T(8,128)(2,1)S(1)}, bf16[1,1024,512]{2,1,0:T(8,128)(2,1)}, u32[]{:S(2)}) copy-start(bf16[1,1024,512]{2,1,0:T(8,128)(2,1)} %param.14) | copy-start | bytes 3145732
  32.9 27.7 %copy-start.10 = (bf16[512,512]{1,0:T(8,128)(2,1)S(1)}, bf16[512,512]{1,0:T(8,128)(2,1)}, u32[]{:S(2)}) copy-start(bf16[512,512]{1,0:T(8,128)(2,1)} %refs_4_.7) | copy-start | bytes 1572868
  46.6 13.9 %collective-permute-start.1 = (bf16[256,512]{1,0:T(8,128)(2,1)S(1)}, bf16[256,512]{1,0:T(8,128)(2,1)S(1)}, u32[]{:S(2)}, u32[]{:S(2)}) collective-permute-start(bf16[256,512]{1,0:T(8,128)(2,1)S(1)} %bitcast.34), channel_id=1, source_target_pairs={{8,0},{16,8},{24,16},{9,1},{17,9},{25,17},{10,2},{18,10},{26,18},{... | collective-permute-start | bytes 786440 | tf_op jit(solution)/shard_map/ppermute | solution.py:550
  47.9 12.6 %collective-permute-start.2 = (s32[1,256]{1,0:T(1,128)S(1)}, s32[1,256]{1,0:T(1,128)S(1)}, u32[]{:S(2)}, u32[]{:S(2)}) collective-permute-start(s32[1,256]{1,0:T(1,128)S(1)} %copy-done.29), channel_id=1, source_target_pairs={{8,0},{16,8},{24,16},{9,1},{17,9},{25,17},{10,2},{18,10},{26,18},{... | collective-permute-start | bytes 3080 | tf_op jit(solution)/shard_map/ppermute | solution.py:550
  64.5 32.2 %collective-permute-start.3 = (bf16[1024,512]{1,0:T(8,128)(2,1)S(1)}, bf16[1024,512]{1,0:T(8,128)(2,1)S(1)}, u32[]{:S(2)}, u32[]{:S(2)}) collective-permute-start(bf16[1024,512]{1,0:T(8,128)(2,1)S(1)} %get-tuple-element.59), channel_id=1, source_target_pairs={{8,0},{16,8},{24,16},{9,1},{17,9},{25,17},{10,2},{18,10},{26,18},{... | collective-permute-start | bytes 3145736 | tf_op jit(solution)/shard_map/ppermute | solution.py:550
  79.1 17.5 %collective-permute-start.4 = (bf16[256,512]{1,0:T(8,128)(2,1)S(1)}, bf16[256,512]{1,0:T(8,128)(2,1)S(1)}, u32[]{:S(2)}, u32[]{:S(2)}) collective-permute-start(bf16[256,512]{1,0:T(8,128)(2,1)S(1)} %bitcast.35), channel_id=1, source_target_pairs={{8,0},{16,8},{24,16},{9,1},{17,9},{25,17},{10,2},{18,10},{26,18},{... | collective-permute-start | bytes 786440 | tf_op jit(solution)/shard_map/ppermute | solution.py:550
  99.0 31.3 %collective-permute-start.5 = (bf16[1024,512]{1,0:T(8,128)(2,1)S(1)}, bf16[1024,512]{1,0:T(8,128)(2,1)S(1)}, u32[]{:S(2)}, u32[]{:S(2)}) collective-permute-start(bf16[1024,512]{1,0:T(8,128)(2,1)S(1)} %get-tuple-element.62), channel_id=1, source_target_pairs={{8,0},{16,8},{24,16},{9,1},{17,9},{25,17},{10,2},{18,10},{26,18},{... | collective-permute-start | bytes 3145736 | tf_op jit(solution)/shard_map/ppermute | solution.py:550
  100.4 29.8 %copy-start.7 = (f32[1024,512]{1,0:T(8,128)S(1)}, f32[1024,512]{1,0:T(8,128)}, u32[]{:S(2)}) copy-start(f32[1024,512]{1,0:T(8,128)} %get-tuple-element.54.refs_2_) | copy-start | bytes 6291460
  113.4 16.8 %collective-permute-start.6 = (bf16[256,512]{1,0:T(8,128)(2,1)S(1)}, bf16[256,512]{1,0:T(8,128)(2,1)S(1)}, u32[]{:S(2)}, u32[]{:S(2)}) collective-permute-start(bf16[256,512]{1,0:T(8,128)(2,1)S(1)} %bitcast.36), channel_id=1, source_target_pairs={{8,0},{16,8},{24,16},{9,1},{17,9},{25,17},{10,2},{18,10},{26,18},{... | collective-permute-start | bytes 786440 | tf_op jit(solution)/shard_map/ppermute | solution.py:550
  139.5 2.4 %collective-permute-start.10 = (bf16[4,192,512]{2,1,0:T(8,128)(2,1)S(1)}, bf16[4,192,512]{2,1,0:T(8,128)(2,1)S(1)}, u32[]{:S(2)}, u32[]{:S(2)}) collective-permute-start(bf16[4,192,512]{2,1,0:T(8,128)(2,1)S(1)} %get-tuple-element.80), channel_id=1, source_target_pairs={{0,1},{1,0},{2,3},{3,2},{4,5},{5,4},{6,7},{7,6},{8,9},{9,8},{10,11... | collective-permute-start | bytes 2359304 | tf_op jit(solution)/shard_map/ppermute | solution.py:755
  139.6 3.4 %collective-permute-start.7 = (bf16[4,192,512]{2,1,0:T(8,128)(2,1)S(1)}, bf16[4,192,512]{2,1,0:T(8,128)(2,1)S(1)}, u32[]{:S(2)}, u32[]{:S(2)}) collective-permute-start(bf16[4,192,512]{2,1,0:T(8,128)(2,1)S(1)} %get-tuple-element.73), channel_id=1, source_target_pairs={{0,1},{1,0},{2,3},{3,2},{4,5},{5,4},{6,7},{7,6},{8,9},{9,8},{10,11... | collective-permute-start | bytes 2359304 | tf_op jit(solution)/shard_map/ppermute | solution.py:755
  142.1 13.6 %collective-permute-start.11 = (bf16[2,192,512]{2,1,0:T(8,128)(2,1)S(1)}, bf16[2,192,512]{2,1,0:T(8,128)(2,1)S(1)}, u32[]{:S(2)}, u32[]{:S(2)}) collective-permute-start(bf16[2,192,512]{2,1,0:T(8,128)(2,1)S(1)} %get-tuple-element.82), channel_id=1, source_target_pairs={{0,4},{1,5},{2,6},{3,7},{4,0},{5,1},{6,2},{7,3},{8,12},{9,13},{10,... | collective-permute-start | bytes 1179656 | tf_op jit(solution)/shard_map/ppermute | solution.py:755
  143.9 16.9 %collective-permute-start.8 = (bf16[2,192,512]{2,1,0:T(8,128)(2,1)}, bf16[2,192,512]{2,1,0:T(8,128)(2,1)}, u32[]{:S(2)}, u32[]{:S(2)}) collective-permute-start(bf16[2,192,512]{2,1,0:T(8,128)(2,1)} %get-tuple-element.75), channel_id=1, source_target_pairs={{0,2},{1,3},{2,0},{3,1},{4,6},{5,7},{6,4},{7,5},{8,10},{9,11},{10,... | collective-permute-start | bytes 1179656 | tf_op jit(solution)/shard_map/ppermute | solution.py:755
  152.1 15.2 %all-to-all-start.4 = ((bf16[8,80,512]{2,1,0:T(8,128)(2,1)}), bf16[8,80,512]{2,1,0:T(8,128)(2,1)S(1)}, u32[]{:S(2)}, u32[]{:S(2)}) async-start(bf16[8,80,512]{2,1,0:T(8,128)(2,1)} %shard_map.191), calls=%async_computation.4 | async-start | bytes 1310720 | tf_op jit(solution)/shard_map/all_to_all | solution.py:747
  157.4 19.0 %copy-start.16 = (f32[1024,512]{1,0:T(8,128)S(1)}, f32[1024,512]{1,0:T(8,128)}, u32[]{:S(2)}) copy-start(f32[1024,512]{1,0:T(8,128)} %copy-done.15) | copy-start | bytes 6291460
  158.8 11.1 %collective-permute-start.12 = (bf16[1,192,512]{2,1,0:T(8,128)(2,1)}, bf16[1,192,512]{2,1,0:T(8,128)(2,1)S(1)}, u32[]{:S(2)}, u32[]{:S(2)}) collective-permute-start(bf16[1,192,512]{2,1,0:T(8,128)(2,1)} %get-tuple-element.84), channel_id=1, source_target_pairs={{0,2},{1,3},{2,0},{3,1},{4,6},{5,7},{6,4},{7,5},{8,10},{9,11},{10,... | collective-permute-start | bytes 589832 | tf_op jit(solution)/shard_map/ppermute | solution.py:755
  162.5 8.2 %collective-permute-start.9 = (bf16[1,192,512]{2,1,0:T(8,128)(2,1)}, bf16[1,192,512]{2,1,0:T(8,128)(2,1)S(1)}, u32[]{:S(2)}, u32[]{:S(2)}) collective-permute-start(bf16[1,192,512]{2,1,0:T(8,128)(2,1)} %get-tuple-element.77), channel_id=1, source_target_pairs={{0,4},{1,5},{2,6},{3,7},{4,0},{5,1},{6,2},{7,3},{8,12},{9,13},{10,... | collective-permute-start | bytes 589832 | tf_op jit(solution)/shard_map/ppermute | solution.py:755
  172.6 16.9 %all-to-all-start.5 = ((bf16[4,112,512]{2,1,0:T(8,128)(2,1)}), bf16[4,112,512]{2,1,0:T(8,128)(2,1)S(1)}, u32[]{:S(2)}, u32[]{:S(2)}) async-start(bf16[4,112,512]{2,1,0:T(8,128)(2,1)} %copy-done.18), calls=%async_computation.5 | async-start | bytes 917504 | tf_op jit(solution)/shard_map/all_to_all | solution.py:783
  (22 other events, 53.2 us)
